TPU v7x, 256 devices: a whole 4x4x8 slice. The times are simulated.
256 devices in a mesh: mkt: 32 (over z, y), draw: 8 (over x, core).
Axes of the slice: x: 4, y: 4, z: 8, core: 2. Of those that a mesh axis runs over, the one named last changes fastest.
Arguments:
- x_char: float32 [1536, 56, 8], P('mkt'), may hold values from -2.5 to 2.5
- nu_draws: float32 [1536, 8, 4096], P('mkt', None, 'draw'), may hold values from -3 to 3
- coef_sigma: float32 [8], replicated, may hold values from 0.3 to 1.2
- log_share: float32 [1536, 56], P('mkt'), may hold values from -7 to -4.5
- counts: int32 [1536], P('mkt'), may hold values from 28 to 56
Outputs:
- mean_util: float32 [1536, 56], P('mkt')
- jacobian: float32 [1536, 56, 56], P(('mkt', 'draw'))
- sup_norms: float32 [3], replicated
Inputs may be any that keep to these rules, and one draw needn't show every extreme that they name: Products 0 to counts - 1 of a market are valid; the other slots are padding.
All inputs are finite; a program needn't handle non-finite values. Where the computation divides by a largest or mean magnitude, that divisor is 1e-20 or more.
Results may differ from a plain program's by a relative error of at most 0.00013.
Values sent between devices are 32-bit elements; how exact they have to be, the bound alone decides.
No kernel may reach another device: no remote copies, remote signals or barrier semaphores. Data moves between devices by JAX's collectives and lax.ppermute only.
A program may use at most 64 MiB of HBM per device.

v0:
```python
import jax
import jax.numpy as jnp
from jax import lax
from jax.experimental import pallas as pl
from jax.experimental.pallas import tpu as pltpu
from jax.sharding import PartitionSpec as P

step_cap = 0.25
epsilon = 1e-06
LOG2E = 1.4426950408889634
VMEM = pl.BlockSpec(memory_space=pltpu.VMEM)
HBM = pl.BlockSpec(memory_space=pltpu.HBM)
SMEM = pl.BlockSpec(memory_space=pltpu.SMEM)
EVERY = ("mkt", "draw")


def pieces(value):
    high = value.astype(jnp.bfloat16).astype(jnp.float32)
    rest = value - high
    middle = rest.astype(jnp.bfloat16).astype(jnp.float32)
    return high, middle, rest - middle


def in_hbm(array):
    return pltpu.with_memory_space_constraint(array, pltpu.HBM)


def params(mebibytes=16):
    return pltpu.CompilerParams(vmem_limit_bytes=mebibytes << 20)


def column(value, slot, lanes=128):
    return jnp.broadcast_to(value[:, slot : slot + 1], (value.shape[0], lanes))


def fill(ref, value):
    tile = jnp.broadcast_to(value, (8, ref.shape[1]))
    for row in range(0, ref.shape[0], 8):
        ref[row : row + 8, :] = tile


def both_starts(copies):
    for copy in copies:
        copy.start()
    return copies


def sigma_levels(sigma_ref, depth, slots):
    level = lax.broadcasted_iota(jnp.int32, (depth, slots), 0)
    sigma = jnp.zeros((depth, slots), jnp.float32)
    for k in range(depth):
        sigma = jnp.where(level == k, sigma_ref[k], sigma)
    return sigma * LOG2E


def left_side(scaled):
    high, middle, low = pieces(scaled)
    left = jnp.concatenate([high, high, middle, high, low, middle], axis=0)
    return jnp.transpose(left).astype(jnp.bfloat16)


def raise_tastes(left, draws):
    high, middle, low = pieces(draws)
    right = jnp.concatenate([high, middle, high, low, high, middle], axis=0)
    return jnp.exp2(jnp.dot(left, right.astype(jnp.bfloat16), preferred_element_type=jnp.float32))


def usable_weights(state_ref, mean_util):
    return jnp.where(state_ref[1] > 0.0, jnp.exp(mean_util), 0.0)


def send_copies(sums_ref, sums):
    for d in range(sums_ref.shape[0]):
        sums_ref[d] = sums


def weight_columns(weights, columns_ref):
    for m in range(columns_ref.shape[0]):
        columns_ref[m] = column(weights, m)


def totals_over(columns_ref, raised_ref):
    markets, slots, draws = raised_ref.shape
    for m in range(markets):
        weight = columns_ref[m]
        total = jnp.zeros((slots, 128), jnp.float32)
        for g in range(0, draws, 128):
            raised = raised_ref[m, :, g : g + 128]
            below = 1.0 + jnp.sum(raised * weight, axis=0, keepdims=True)
            total = total + raised * (1.0 / below)
        columns_ref[m] = total


def packed_sums(totals_ref):
    markets, slots = totals_ref.shape[:2]
    lane = lax.broadcasted_iota(jnp.int32, (32, 128), 1)
    sums = jnp.zeros((32, 128), jnp.float32)
    upper = jnp.zeros((32, 128), jnp.float32)
    for m in range(markets):
        one = jnp.sum(totals_ref[m], axis=1, keepdims=True)
        rest = jnp.concatenate([one[32:slots], jnp.zeros((64 - slots, 1), jnp.float32)], axis=0)
        sums = jnp.where(lane == m, one[0:32], sums)
        upper = jnp.where(lane == m + 64, rest, upper)
    return jnp.where(lane < 64, sums, upper)


def start_kernel(counts_hbm, sigma_hbm, log_share_hbm, x_hbm, nu_hbm, state_ref, sums_ref, nu_ref, kept_ref, counts_ref, sigma_ref, rows_ref, log_share_ref, x_ref, left_ref, raised_ref, columns_ref, sems):
    markets, slots = log_share_hbm.shape
    depth = x_hbm.shape[1]
    chunk = markets // 4
    small = both_starts(
        [
            pltpu.make_async_copy(x_hbm, x_ref, sems.at[0]),
            pltpu.make_async_copy(sigma_hbm, sigma_ref, sems.at[1]),
            pltpu.make_async_copy(log_share_hbm, log_share_ref, sems.at[2]),
            pltpu.make_async_copy(counts_hbm, counts_ref, sems.at[3]),
        ]
    )
    large = both_starts(
        [
            pltpu.make_async_copy(nu_hbm.at[pl.ds(c * chunk, chunk)], nu_ref.at[pl.ds(c * chunk, chunk)], sems.at[4 + c])
            for c in range(4)
        ]
    )
    rows_ref[...] = jnp.zeros_like(rows_ref)
    for copy in small:
        copy.wait()
    sigma = sigma_levels(sigma_ref, depth, slots)
    for m in range(markets):
        left_ref[m] = left_side(x_ref[m] * sigma)
    base = lax.axis_index("draw") * kept_ref.shape[0]
    for m in range(kept_ref.shape[0]):
        kept_ref[m] = left_ref[base + m]
    rows_ref[0:markets, 0:slots] = log_share_ref[...]
    log_share = jnp.transpose(rows_ref[...])[0:slots, :]
    slot = lax.broadcasted_iota(jnp.int32, (slots, 128), 0)
    lane = lax.broadcasted_iota(jnp.int32, (8, 128), 1)
    count = jnp.zeros((8, 128), jnp.int32)
    for m in range(markets):
        count = jnp.where(lane == m, counts_ref[m], count)
    usable = slot < jnp.broadcast_to(count[0:1, :], (slots, 128))
    inside = jnp.sum(jnp.where(usable, jnp.exp(log_share), 0.0), axis=0, keepdims=True)
    mean_util = jnp.where(usable, log_share - jnp.log(1.0 - inside), 0.0)
    state_ref[0] = log_share
    state_ref[1] = jnp.where(usable, 1.0, 0.0)
    state_ref[2] = mean_util
    weight_columns(jnp.where(usable, jnp.exp(mean_util), 0.0), columns_ref)
    for copy in large:
        copy.wait()
    for m in range(markets):
        raised_ref[m] = raise_tastes(left_ref[m], nu_ref[m])
    totals_over(columns_ref, raised_ref)
    send_copies(sums_ref, packed_sums(columns_ref))


def stage_kernel(nu_ref, partner_ref, *sends):
    own = sends[0].shape[1]
    mine = lax.axis_index("draw")
    for k, send in enumerate(sends):
        first = (mine ^ (2 * (k + 1))) * own
        for m in range(own):
            send[0, m] = nu_ref[first + m]
            send[1, m] = partner_ref[first + m]


def keep_kernel(own, all_ref, kept_ref):
    slots = all_ref.shape[1]
    shift = 128 - lax.axis_index("draw") * own
    kept = lax.broadcasted_iota(jnp.int32, (slots, 8), 1) < own
    for p in range(3):
        kept_ref[p] = jnp.where(kept, pltpu.roll(all_ref[p], shift, axis=1)[:, 0:8], 0.0)


def change_kernel(inverse, own, sums_ref, all_ref, kept_ref, state_ref, peak_ref):
    mine = lax.axis_index("draw")
    total = sums_ref[0]
    for d in range(1, sums_ref.shape[0]):
        total = total + sums_ref[d]
    slots = all_ref.shape[1]
    sums = jnp.concatenate([total, pltpu.roll(total, 64, axis=1)[0 : slots - 32]], axis=0)
    usable = all_ref[1] > 0.0
    shares = sums * usable_weights(all_ref, all_ref[2]) * inverse
    change = jnp.where(usable, all_ref[0] - jnp.log(jnp.where(usable, shares, 1.0)), 0.0)
    fill(peak_ref, jnp.max(jnp.abs(change)))
    kept = lax.broadcasted_iota(jnp.int32, (slots, 8), 1) < own
    for p in range(3):
        state_ref[p] = kept_ref[p]
    state_ref[3] = jnp.where(kept, pltpu.roll(change, 128 - mine * own, axis=1)[:, 0:8], 0.0)
    state_ref[4] = jnp.zeros((slots, 8), jnp.float32)


def moved(turn, peaks_ref, state_ref):
    largest = jnp.max(peaks_ref[...])
    step = jnp.minimum(1.0, step_cap / (largest + epsilon))
    row = lax.broadcasted_iota(jnp.int32, state_ref.shape[1:], 0)
    return step, state_ref[2] + step * state_ref[3], jnp.where(row == turn, largest, state_ref[4])


def next_change(turn, peaks_ref, state_ref, out_ref, raised_ref, columns_ref):
    own, _, draws = raised_ref.shape
    _, mean_util, norms = moved(turn, peaks_ref, state_ref)
    usable = state_ref[1] > 0.0
    weights = jnp.where(usable, jnp.exp(mean_util), 0.0)
    weight_columns(weights, columns_ref)
    totals_over(columns_ref, raised_ref)
    lane = lax.broadcasted_iota(jnp.int32, weights.shape, 1)
    sums = jnp.ones(weights.shape, jnp.float32)
    for m in range(own):
        sums = jnp.where(lane == m, jnp.sum(columns_ref[m], axis=1, keepdims=True), sums)
    shares = sums * weights * (1.0 / draws)
    change = jnp.where(usable, state_ref[0] - jnp.log(jnp.where(usable, shares, 1.0)), 0.0)
    out_ref[0] = state_ref[0]
    out_ref[1] = state_ref[1]
    out_ref[2] = mean_util
    out_ref[3] = change
    out_ref[4] = norms
    return mean_util, change


def second_kernel(peaks_ref, state_ref, left_ref, nu_ref, partner_ref, *refs):
    received = refs[:3]
    raised_ref, out_ref, peak_ref, columns_ref = refs[3:]
    own = raised_ref.shape[0]
    base = lax.axis_index("draw") * own
    sources = [nu_ref.at[pl.ds(base, own)], partner_ref.at[pl.ds(base, own)]]
    for ref in received:
        sources += [ref.at[0], ref.at[1]]
    span = nu_ref.shape[2]
    for m in range(own):
        for s, source in enumerate(sources):
            raised_ref[m, :, s * span : (s + 1) * span] = raise_tastes(left_ref[m], source[m])
    _, change = next_change(0, peaks_ref, state_ref, out_ref, raised_ref, columns_ref)
    fill(peak_ref, jnp.max(jnp.abs(change)))


def as_rows(value):
    padded = jnp.concatenate([value, jnp.zeros((128 - value.shape[0], 8), jnp.float32)], axis=0)
    return jnp.transpose(padded)


def third_kernel(peaks_ref, state_ref, raised_ref, out_ref, rows_ref, columns_ref):
    mean_util, change = next_change(1, peaks_ref, state_ref, out_ref, raised_ref, columns_ref)
    send_copies(rows_ref, jnp.concatenate([as_rows(mean_util), as_rows(change)], axis=0))


def join_kernel(rows_ref, peak_ref):
    largest = jnp.abs(rows_ref[0, 8:16, :])
    for d in range(1, rows_ref.shape[0]):
        largest = jnp.maximum(largest, jnp.abs(rows_ref[d, 8:16, :]))
    fill(peak_ref, jnp.max(largest))


def final_kernel(peaks_ref, state_ref, rows_ref, raised_ref, jacobian_ref, mean_ref, norms_ref, both_ref, columns_ref, product_ref):
    own, slots, draws = raised_ref.shape
    step, mean_util, norms = moved(2, peaks_ref, state_ref)
    usable = state_ref[1]
    weight_columns(jnp.where(usable > 0.0, jnp.exp(mean_util), 0.0), columns_ref)
    usable_rows = as_rows(usable)
    for t in range(3):
        norms_ref[t] = jnp.max(norms[t : t + 1, :])
    for d in range(rows_ref.shape[0]):
        rows = rows_ref[d, 0:8, :] + step * rows_ref[d, 8:16, :]
        mean_ref[d * own : (d + 1) * own, :] = rows[0:own, 0:slots]
    padding = jnp.zeros((64 - slots, 128), jnp.float32)
    for m in range(own):
        weight = columns_ref[m]
        total = jnp.zeros((slots, 128), jnp.float32)
        buffer = m % 2
        for g in range(0, draws, 128):
            raised = raised_ref[m, :, g : g + 128] * weight
            chance = raised * (1.0 / (1.0 + jnp.sum(raised, axis=0, keepdims=True)))
            total = total + chance
            padded = jnp.concatenate([chance, padding], axis=0)
            high = padded.astype(jnp.bfloat16)
            low = (padded - high.astype(jnp.float32)).astype(jnp.bfloat16)
            both_ref[buffer, 0:64, g : g + 128] = high
            both_ref[buffer, 64:128, g : g + 128] = low
        columns_ref[m] = total
        product_ref[m] = lax.dot_general(
            both_ref[buffer],
            both_ref[buffer, 0:64, :],
            (((1,), (1,)), ((), ())),
            preferred_element_type=jnp.float32,
        )
    row = lax.broadcasted_iota(jnp.int32, (slots, slots), 0)
    col = lax.broadcasted_iota(jnp.int32, (slots, slots), 1)
    identity = jnp.where(row == col, 1.0, 0.0)
    for m in range(own):
        product = product_ref[m]
        crossed = product[64:128]
        cross = (product[0:64] + crossed + jnp.transpose(crossed))[0:slots, 0:slots]
        shares = jnp.sum(columns_ref[m], axis=1, keepdims=True)
        valid = column(usable, m, slots) > 0.0
        paired = valid & (usable_rows[m : m + 1, 0:slots] > 0.0)
        divisor = jnp.where(valid, shares, 1.0)
        jacobian_ref[m] = jnp.where(paired, identity - cross / divisor, 0.0)


def contract(x_char, nu_draws, coef_sigma, log_share, counts):
    markets, slots = log_share.shape
    depth, span = nu_draws.shape[1:]
    draw_count, mkt_count, every = (lax.axis_size(axis) for axis in ("draw", "mkt", EVERY))
    own = markets // draw_count
    draws = span * draw_count
    f32, bf16 = jnp.float32, jnp.bfloat16
    shape = lambda *sizes: jax.ShapeDtypeStruct(sizes, f32)
    state_shape = shape(5, slots, 8)
    columns = pltpu.VMEM((own, slots, 128), f32)

    def exchange(array, distance):
        return lax.ppermute(array, "draw", [(d, d ^ distance) for d in range(draw_count)])

    def peaks_of(peak, axis):
        count = peak.shape[0]
        return lax.all_to_all(peak.reshape(count, 1, 128), axis, 0, 0, tiled=True).reshape(count, 128)

    partner = exchange(nu_draws, 1)
    x_rows, sigma, nu_hbm = in_hbm(jnp.transpose(x_char, (0, 2, 1))), in_hbm(coef_sigma), in_hbm(nu_draws)
    all_state, sums, nu_near, left = pl.pallas_call(
        start_kernel,
        out_shape=(shape(3, slots, 128), shape(draw_count, 32, 128), shape(markets, depth, span), jax.ShapeDtypeStruct((own, slots, 6 * depth), bf16)),
        in_specs=[HBM] * 5,
        out_specs=(VMEM,) * 4,
        scratch_shapes=[
            pltpu.SMEM((markets,), jnp.int32),
            pltpu.SMEM((depth,), f32),
            pltpu.VMEM((128, 128), f32),
            pltpu.VMEM((markets, slots), f32),
            pltpu.VMEM((markets, depth, slots), f32),
            pltpu.VMEM((markets, slots, 6 * depth), bf16),
            pltpu.VMEM((markets, slots, span), f32),
            pltpu.VMEM((markets, slots, 128), f32),
            pltpu.SemaphoreType.DMA((8,)),
        ],
        compiler_params=params(),
        name="start",
    )(in_hbm(counts), sigma, in_hbm(log_share), x_rows, nu_hbm)
    sends = pl.pallas_call(
        stage_kernel,
        out_shape=(shape(2, own, depth, span),) * 3,
        in_specs=[VMEM] * 2,
        out_specs=(VMEM,) * 3,
        compiler_params=params(),
        name="stage",
    )(nu_near, partner)
    received = []
    for k, send in enumerate(sends):
        received.append(exchange(send, 2 * (k + 1)))
    sums = lax.all_to_all(sums, "draw", 0, 0, tiled=True)
    kept = pl.pallas_call(
        lambda *refs: keep_kernel(own, *refs),
        out_shape=shape(3, slots, 8),
        in_specs=[VMEM],
        out_specs=VMEM,
        compiler_params=params(),
        name="keep",
    )(all_state)
    state, peak = pl.pallas_call(
        lambda *refs: change_kernel(1.0 / draws, own, *refs),
        out_shape=(state_shape, shape(mkt_count, 128)),
        in_specs=[VMEM] * 3,
        out_specs=(VMEM,) * 2,
        compiler_params=params(),
        name="change",
    )(sums, all_state, kept)
    peaks = peaks_of(peak, "mkt")
    raised, state, peak = pl.pallas_call(
        second_kernel,
        out_shape=(shape(own, slots, draws), state_shape, shape(every, 128)),
        in_specs=[VMEM] * 8,
        out_specs=(VMEM,) * 3,
        scratch_shapes=[columns],
        compiler_params=params(),
        name="second",
    )(peaks, state, left, nu_near, partner, *received)
    state, rows = pl.pallas_call(
        third_kernel,
        out_shape=(state_shape, shape(draw_count, 16, 128)),
        in_specs=[VMEM] * 3,
        out_specs=(VMEM,) * 2,
        scratch_shapes=[columns],
        compiler_params=params(),
        name="third",
    )(peaks_of(peak, EVERY), state, raised)
    rows = lax.all_to_all(rows, "draw", 0, 0, tiled=True)
    peak = pl.pallas_call(
        join_kernel,
        out_shape=shape(mkt_count, 128),
        in_specs=[VMEM],
        out_specs=VMEM,
        compiler_params=params(),
        name="join",
    )(rows)
    jacobian, mean_util, norms = pl.pallas_call(
        final_kernel,
        out_shape=(shape(own, slots, slots), shape(markets, slots), shape(3)),
        in_specs=[VMEM] * 4,
        out_specs=(VMEM, VMEM, SMEM),
        scratch_shapes=[pltpu.VMEM((2, 128, draws), bf16), columns, pltpu.VMEM((own, 128, 64), f32)],
        compiler_params=params(),
        name="final",
    )(peaks_of(peak, "mkt"), state, rows, raised)
    return (mean_util, jacobian, norms)


def solution(mesh):
    return jax.shard_map(
        contract,
        mesh=mesh,
        in_specs=(P("mkt", None, None), P("mkt", None, "draw"), P(), P("mkt", None), P("mkt")),
        out_specs=(P("mkt", None), P(("mkt", "draw"), None, None), P()),
        check_vma=False,
    )
```

profile of v0, /device:TPU:1, one launch (start us, length us, event | category | flops | bytes accessed | tf_op | source)
XLA Modules:
  0.0 92.2 jit_solution(17773819745240852757)
XLA Ops:
  0.6 3.3 %collective-permute-start = (f32[48,8,512]{2,1,0:T(8,128)}, f32[48,8,512]{2,1,0:T(8,128)S(1)}, u32[]{:S(2)}, u32[]{:S(2)}) collective-permute-start(f32[48,8,512]{2,1,0:T(8,128)} %nu_hbm.1), channel_id=1, source_target_pairs={{0,1},{1,0},{2,3},{3,2},{4,5},{5,4},{6,7},{7,6},{8,9},{9,8},{10,11... | collective-permute-start | bytes 2359304 | tf_op jit(solution)/shard_map/ppermute | solution.py:311
  3.9 4.6 %start.1 = (f32[3,56,128]{2,1,0:T(8,128)S(1)}, f32[8,32,128]{2,1,0:T(8,128)}, f32[48,8,512]{2,1,0:T(8,128)S(1)}, bf16[6,56,48]{2,1,0:T(8,128)(2,1)S(1)}) custom-call(s32[48]{0:T(128)} %counts_hbm.1, f32[8]{0:T(128)} %sigma_hbm.1, f32[48,56]{1,0:T(8,128)} %log_share_hbm.1, f32[48,8,56]{2,1,0:T(8,128)} %bitcast.19, f32[48,8,512]{2,1,0:T(8,128)} %nu_hbm.1), custom_call_target="tpu_custom_call" | custom-call | tf_op jit(solution)/shard_map/start/pallas_call | solution.py:319
  8.5 0.0 collective-permute-done.partner_ref
  8.6 0.1 collective-permute-start.1
  8.7 1.9 %collective-permute-start.2 = (f32[2,6,8,512]{3,2,1,0:T(8,128)S(1)}, f32[2,6,8,512]{3,2,1,0:T(8,128)S(1)}, u32[]{:S(2)}, u32[]{:S(2)}) collective-permute-start(f32[2,6,8,512]{3,2,1,0:T(8,128)S(1)} %get-tuple-element.27), channel_id=1, source_target_pairs={{0,4},{1,5},{2,6},{3,7},{4,0},{5,1},{6,2},{7,3},{8,12},{9,13},{10,... | collective-permute-start | bytes 589832 | tf_op jit(solution)/shard_map/ppermute | solution.py:311
  10.7 1.9 %collective-permute-start.3 = (f32[2,6,8,512]{3,2,1,0:T(8,128)S(1)}, f32[2,6,8,512]{3,2,1,0:T(8,128)S(1)}, u32[]{:S(2)}, u32[]{:S(2)}) collective-permute-start(f32[2,6,8,512]{3,2,1,0:T(8,128)S(1)} %get-tuple-element.28), channel_id=1, source_target_pairs={{0,6},{1,7},{2,4},{3,5},{4,2},{5,3},{6,0},{7,1},{8,14},{9,15},{10,... | collective-permute-start | bytes 589832 | tf_op jit(solution)/shard_map/ppermute | solution.py:311
  12.6 4.1 %all-to-all-start = ((f32[8,32,128]{2,1,0:T(8,128)}), f32[8,32,128]{2,1,0:T(8,128)S(1)}, u32[]{:S(2)}, u32[]{:S(2)}) async-start(f32[8,32,128]{2,1,0:T(8,128)} %get-tuple-element.20), calls=%async_computation | async-start | bytes 262144 | tf_op jit(solution)/shard_map/all_to_all | solution.py:349
  16.7 0.1 keep.1.refs_2_
  16.8 7.3 %all-to-all-done.refs_0_ = f32[8,32,128]{2,1,0:T(8,128)S(1)} async-done(((f32[8,32,128]{2,1,0:T(8,128)}), f32[8,32,128]{2,1,0:T(8,128)S(1)}, u32[]{:S(2)}, u32[]{:S(2)}) %all-to-all-start) | async-done | bytes 131104 | tf_op jit(solution)/shard_map/all_to_all | solution.py:349
  24.1 0.2 change.1
  24.3 19.6 %all_to_all.25 = f32[32,1,128]{2,1,0:T(1,128)S(1)} all-to-all(f32[32,1,128]{2,1,0:T(1,128)S(1)} %bitcast.18), channel_id=1, replica_groups=mesh['mkt'=32,'draw'=8] {'mkt'}, dimensions={0} | all-to-all | bytes 32768 | tf_op jit(solution)/shard_map/all_to_all | solution.py:315
  43.9 0.0 collective-permute-done.1.refs_0_
  43.9 0.0 collective-permute-done.2.refs_1_
  43.9 0.0 collective-permute-done.3.refs_2_
  43.9 2.1 %second.1 = (f32[6,56,4096]{2,1,0:T(8,128)S(1)}, f32[5,56,8]{2,1,0:T(8,128)S(1)}, f32[256,128]{1,0:T(8,128)S(1)}) custom-call(f32[32,128]{1,0:T(8,128)S(1)} %bitcast.15, f32[5,56,8]{2,1,0:T(8,128)S(1)} %get-tuple-element.23.state_ref, bf16[6,56,48]{2,1,0:T(8,128)(2,1)S(1)} %get-tuple-element.24.left_ref, f32[48,8,512]{2,1,0:T(8,128)S(1)} %get-tuple-element.25.nu_ref, ...), custom_call_target="tpu_custom_call" | custom-call | tf_op jit(solution)/shard_map/second/pallas_call | solution.py:367
  46.0 20.0 %all_to_all.26 = f32[256,1,128]{2,1,0:T(1,128)S(1)} all-to-all(f32[256,1,128]{2,1,0:T(1,128)S(1)} %bitcast.14), channel_id=1, replica_groups=mesh['mkt'=32,'draw'=8] {'mkt','draw'}, dimensions={0} | all-to-all | bytes 262144 | tf_op jit(solution)/shard_map/all_to_all | solution.py:315
  66.0 1.5 %third.1 = (f32[5,56,8]{2,1,0:T(8,128)S(1)}, f32[8,16,128]{2,1,0:T(8,128)S(1)}) custom-call(f32[256,128]{1,0:T(8,128)S(1)} %bitcast.13, f32[5,56,8]{2,1,0:T(8,128)S(1)} %get-tuple-element.30.state_ref, f32[6,56,4096]{2,1,0:T(8,128)S(1)} %get-tuple-element.31.raised_ref), custom_call_target="tpu_custom_call" | custom-call | tf_op jit(solution)/shard_map/third/pallas_call | solution.py:376
  67.5 8.0 %all_to_all.27.rows_ref = f32[8,16,128]{2,1,0:T(8,128)S(1)} all-to-all(f32[8,16,128]{2,1,0:T(8,128)S(1)} %get-tuple-element.32), channel_id=1, replica_groups=mesh['mkt'=32,'draw'=8] {'draw'}, dimensions={0} | all-to-all | bytes 131072 | tf_op jit(solution)/shard_map/all_to_all | solution.py:385
  75.5 0.1 join.1
  75.6 11.8 %all_to_all.28 = f32[32,1,128]{2,1,0:T(1,128)S(1)} all-to-all(f32[32,1,128]{2,1,0:T(1,128)S(1)} %bitcast.17), channel_id=1, replica_groups=mesh['mkt'=32,'draw'=8] {'mkt'}, dimensions={0} | all-to-all | bytes 32768 | tf_op jit(solution)/shard_map/all_to_all | solution.py:315
  87.4 4.6 %final.1 = (f32[6,56,56]{2,1,0:T(8,128)}, f32[48,56]{1,0:T(8,128)}, f32[3]{0:T(128)}) custom-call(f32[32,128]{1,0:T(8,128)S(1)} %bitcast.16, f32[5,56,8]{2,1,0:T(8,128)S(1)} %get-tuple-element.33.state_ref, f32[8,16,128]{2,1,0:T(8,128)S(1)} %all_to_all.27.rows_ref, f32[6,56,4096]{2,1,0:T(8,128)S(1)} %get-tuple-element.31.raised_ref), custom_call_target="tpu_custom_call" | custom-call | tf_op jit(solution)/shard_map/final/pallas_call | solution.py:394
  (1 shorter events, 0.0 us)
Async XLA Ops:
  0.6 7.9 %collective-permute-start = (f32[48,8,512]{2,1,0:T(8,128)}, f32[48,8,512]{2,1,0:T(8,128)S(1)}, u32[]{:S(2)}, u32[]{:S(2)}) collective-permute-start(f32[48,8,512]{2,1,0:T(8,128)} %nu_hbm.1), channel_id=1, source_target_pairs={{0,1},{1,0},{2,3},{3,2},{4,5},{5,4},{6,7},{7,6},{8,9},{9,8},{10,11... | collective-permute-start | bytes 2359304 | tf_op jit(solution)/shard_map/ppermute | solution.py:311
  8.6 35.3 %collective-permute-start.1 = (f32[2,6,8,512]{3,2,1,0:T(8,128)S(1)}, f32[2,6,8,512]{3,2,1,0:T(8,128)S(1)}, u32[]{:S(2)}, u32[]{:S(2)}) collective-permute-start(f32[2,6,8,512]{3,2,1,0:T(8,128)S(1)} %get-tuple-element.26), channel_id=1, source_target_pairs={{0,2},{1,3},{2,0},{3,1},{4,6},{5,7},{6,4},{7,5},{8,10},{9,11},{10,... | collective-permute-start | bytes 589832 | tf_op jit(solution)/shard_map/ppermute | solution.py:311
  8.7 35.2 %collective-permute-start.2 = (f32[2,6,8,512]{3,2,1,0:T(8,128)S(1)}, f32[2,6,8,512]{3,2,1,0:T(8,128)S(1)}, u32[]{:S(2)}, u32[]{:S(2)}) collective-permute-start(f32[2,6,8,512]{3,2,1,0:T(8,128)S(1)} %get-tuple-element.27), channel_id=1, source_target_pairs={{0,4},{1,5},{2,6},{3,7},{4,0},{5,1},{6,2},{7,3},{8,12},{9,13},{10,... | collective-permute-start | bytes 589832 | tf_op jit(solution)/shard_map/ppermute | solution.py:311
  10.7 33.2 %collective-permute-start.3 = (f32[2,6,8,512]{3,2,1,0:T(8,128)S(1)}, f32[2,6,8,512]{3,2,1,0:T(8,128)S(1)}, u32[]{:S(2)}, u32[]{:S(2)}) collective-permute-start(f32[2,6,8,512]{3,2,1,0:T(8,128)S(1)} %get-tuple-element.28), channel_id=1, source_target_pairs={{0,6},{1,7},{2,4},{3,5},{4,2},{5,3},{6,0},{7,1},{8,14},{9,15},{10,... | collective-permute-start | bytes 589832 | tf_op jit(solution)/shard_map/ppermute | solution.py:311
  12.6 11.5 %all-to-all-start = ((f32[8,32,128]{2,1,0:T(8,128)}), f32[8,32,128]{2,1,0:T(8,128)S(1)}, u32[]{:S(2)}, u32[]{:S(2)}) async-start(f32[8,32,128]{2,1,0:T(8,128)} %get-tuple-element.20), calls=%async_computation | async-start | bytes 262144 | tf_op jit(solution)/shard_map/all_to_all | solution.py:349
where the time goes:
time: 92.5 us; the launch traced here: 92.2 us
  blocking collectives  59.3 us (64%)
  Pallas kernels  13.3 us (14%)
  starting transfers between devices  11.3 us (12%)
  waiting for transfers between devices  7.29 us (8%)
    all_to_all x3, blocking collectives, peaks_of(): lax.all_to_all(peak.reshape(count, 1, 128), axis, 0, 0, tiled=True)  51.4 us
    all_to_all x1, blocking collectives, contract(): rows = lax.all_to_all(rows, 'draw', 0, 0, tiled=True)  7.97 us
    all_to_all x1, waiting for transfers between devices, contract(): sums = lax.all_to_all(sums, 'draw', 0, 0, tiled=True)  7.28 us
    ppermute x4, starting transfers between devices, exchange(): lax.ppermute(array, 'draw', [(d, d ^ distance) for d in range(draw_count)])  7.23 us
    pallas_call x1, Pallas kernels, contract(): pl.pallas_call(final_kernel, out_shape=(shape(own, slots, slots), shape(m...  4.64 us
    pallas_call x1, Pallas kernels, contract(): pl.pallas_call(start_kernel, out_shape=(shape(3, slots, 128), shape(draw_...  4.62 us
    all_to_all x1, starting transfers between devices, contract(): sums = lax.all_to_all(sums, 'draw', 0, 0, tiled=True)  4.12 us
    pallas_call x1, Pallas kernels, contract(): pl.pallas_call(second_kernel, out_shape=(shape(own, slots, draws), state_...  2.06 us
  transfers between devices with their start and end apart: 5, of which 1 were waited for; matrix products, arithmetic and copies ran while one was open for 0% of the time, Pallas kernels for 5%

commit v1 on v0

--- a/solution.py
+++ b/solution.py
@@ -56,7 +56,7 @@
 def left_side(scaled):
     high, middle, low = pieces(scaled)
     left = jnp.concatenate([high, high, middle, high, low, middle], axis=0)
-    return jnp.transpose(left).astype(jnp.bfloat16)
+    return jnp.transpose(left.astype(jnp.bfloat16))
 
 
 def raise_tastes(left, draws):
@@ -79,16 +79,38 @@
         columns_ref[m] = column(weights, m)
 
 
-def totals_over(columns_ref, raised_ref):
+def eights(markets, draws):
+    units = [(m, g) for m in markets for g in range(0, draws, 128)]
+    return [units[u : u + 8] for u in range(0, len(units), 8)]
+
+
+def inverse_rows(units, slot, columns_ref, raised_ref, parts_ref, inverse_ref):
+    slots = raised_ref.shape[1]
+    for u, (m, g) in enumerate(units):
+        part = raised_ref[m, 0:8, g : g + 128] * columns_ref[m, 0:8, :]
+        for j in range(8, slots, 8):
+            part = part + raised_ref[m, j : j + 8, g : g + 128] * columns_ref[m, j : j + 8, :]
+        parts_ref[slot, 8 * u : 8 * u + 8, :] = part
+    below = parts_ref[slot, pl.ds(0, 8, stride=8), :] + 1.0
+    for j in range(1, 8):
+        below = below + parts_ref[slot, pl.ds(j, 8, stride=8), :]
+    inverse_ref[slot] = 1.0 / below
+
+
+def totals_over(columns_ref, raised_ref, parts_ref, inverse_ref, totals_ref):
     markets, slots, draws = raised_ref.shape
-    for m in range(markets):
-        weight = columns_ref[m]
-        total = jnp.zeros((slots, 128), jnp.float32)
-        for g in range(0, draws, 128):
-            raised = raised_ref[m, :, g : g + 128]
-            below = 1.0 + jnp.sum(raised * weight, axis=0, keepdims=True)
-            total = total + raised * (1.0 / below)
-        columns_ref[m] = total
+    for b, units in enumerate(eights(range(markets), draws)):
+        slot = b % parts_ref.shape[0]
+        inverse_rows(units, slot, columns_ref, raised_ref, parts_ref, inverse_ref)
+        for m in sorted(set(m for m, _ in units)):
+            total = jnp.zeros((slots, 128), jnp.float32)
+            for u, (other, g) in enumerate(units):
+                if other == m:
+                    total = total + raised_ref[m, :, g : g + 128] * inverse_ref[slot, u : u + 1, :]
+            if any(g == 0 for other, g in units if other == m):
+                totals_ref[m] = total
+            else:
+                totals_ref[m] += total
 
 
 def packed_sums(totals_ref):
@@ -104,7 +126,7 @@
     return jnp.where(lane < 64, sums, upper)
 
 
-def start_kernel(counts_hbm, sigma_hbm, log_share_hbm, x_hbm, nu_hbm, state_ref, sums_ref, nu_ref, kept_ref, counts_ref, sigma_ref, rows_ref, log_share_ref, x_ref, left_ref, raised_ref, columns_ref, sems):
+def start_kernel(counts_hbm, sigma_hbm, log_share_hbm, x_hbm, nu_hbm, state_ref, sums_ref, nu_ref, kept_ref, counts_ref, sigma_ref, rows_ref, log_share_ref, x_ref, left_ref, raised_ref, columns_ref, totals_ref, parts_ref, inverse_ref, sems):
     markets, slots = log_share_hbm.shape
     depth = x_hbm.shape[1]
     chunk = markets // 4
@@ -149,8 +171,8 @@
         copy.wait()
     for m in range(markets):
         raised_ref[m] = raise_tastes(left_ref[m], nu_ref[m])
-    totals_over(columns_ref, raised_ref)
-    send_copies(sums_ref, packed_sums(columns_ref))
+    totals_over(columns_ref, raised_ref, parts_ref, inverse_ref, totals_ref)
+    send_copies(sums_ref, packed_sums(totals_ref))
 
 
 def stage_kernel(nu_ref, partner_ref, *sends):
@@ -196,17 +218,17 @@
     return step, state_ref[2] + step * state_ref[3], jnp.where(row == turn, largest, state_ref[4])
 
 
-def next_change(turn, peaks_ref, state_ref, out_ref, raised_ref, columns_ref):
+def next_change(turn, peaks_ref, state_ref, out_ref, raised_ref, columns_ref, totals_ref, *eight):
     own, _, draws = raised_ref.shape
     _, mean_util, norms = moved(turn, peaks_ref, state_ref)
     usable = state_ref[1] > 0.0
     weights = jnp.where(usable, jnp.exp(mean_util), 0.0)
     weight_columns(weights, columns_ref)
-    totals_over(columns_ref, raised_ref)
+    totals_over(columns_ref, raised_ref, *eight, totals_ref)
     lane = lax.broadcasted_iota(jnp.int32, weights.shape, 1)
     sums = jnp.ones(weights.shape, jnp.float32)
     for m in range(own):
-        sums = jnp.where(lane == m, jnp.sum(columns_ref[m], axis=1, keepdims=True), sums)
+        sums = jnp.where(lane == m, jnp.sum(totals_ref[m], axis=1, keepdims=True), sums)
     shares = sums * weights * (1.0 / draws)
     change = jnp.where(usable, state_ref[0] - jnp.log(jnp.where(usable, shares, 1.0)), 0.0)
     out_ref[0] = state_ref[0]
@@ -219,7 +241,7 @@
 
 def second_kernel(peaks_ref, state_ref, left_ref, nu_ref, partner_ref, *refs):
     received = refs[:3]
-    raised_ref, out_ref, peak_ref, columns_ref = refs[3:]
+    raised_ref, out_ref, peak_ref, *scratch = refs[3:]
     own = raised_ref.shape[0]
     base = lax.axis_index("draw") * own
     sources = [nu_ref.at[pl.ds(base, own)], partner_ref.at[pl.ds(base, own)]]
@@ -229,7 +251,7 @@
     for m in range(own):
         for s, source in enumerate(sources):
             raised_ref[m, :, s * span : (s + 1) * span] = raise_tastes(left_ref[m], source[m])
-    _, change = next_change(0, peaks_ref, state_ref, out_ref, raised_ref, columns_ref)
+    _, change = next_change(0, peaks_ref, state_ref, out_ref, raised_ref, *scratch)
     fill(peak_ref, jnp.max(jnp.abs(change)))
 
 
@@ -238,8 +260,8 @@
     return jnp.transpose(padded)
 
 
-def third_kernel(peaks_ref, state_ref, raised_ref, out_ref, rows_ref, columns_ref):
-    mean_util, change = next_change(1, peaks_ref, state_ref, out_ref, raised_ref, columns_ref)
+def third_kernel(peaks_ref, state_ref, raised_ref, out_ref, rows_ref, *scratch):
+    mean_util, change = next_change(1, peaks_ref, state_ref, out_ref, raised_ref, *scratch)
     send_copies(rows_ref, jnp.concatenate([as_rows(mean_util), as_rows(change)], axis=0))
 
 
@@ -250,7 +272,7 @@
     fill(peak_ref, jnp.max(largest))
 
 
-def final_kernel(peaks_ref, state_ref, rows_ref, raised_ref, jacobian_ref, mean_ref, norms_ref, both_ref, columns_ref, product_ref):
+def final_kernel(peaks_ref, state_ref, rows_ref, raised_ref, jacobian_ref, mean_ref, norms_ref, even_ref, odd_ref, columns_ref, product_ref, parts_ref, inverse_ref):
     own, slots, draws = raised_ref.shape
     step, mean_util, norms = moved(2, peaks_ref, state_ref)
     usable = state_ref[1]
@@ -261,27 +283,36 @@
     for d in range(rows_ref.shape[0]):
         rows = rows_ref[d, 0:8, :] + step * rows_ref[d, 8:16, :]
         mean_ref[d * own : (d + 1) * own, :] = rows[0:own, 0:slots]
-    padding = jnp.zeros((64 - slots, 128), jnp.float32)
-    for m in range(own):
-        weight = columns_ref[m]
-        total = jnp.zeros((slots, 128), jnp.float32)
-        buffer = m % 2
-        for g in range(0, draws, 128):
-            raised = raised_ref[m, :, g : g + 128] * weight
-            chance = raised * (1.0 / (1.0 + jnp.sum(raised, axis=0, keepdims=True)))
-            total = total + chance
-            padded = jnp.concatenate([chance, padding], axis=0)
-            high = padded.astype(jnp.bfloat16)
-            low = (padded - high.astype(jnp.float32)).astype(jnp.bfloat16)
-            both_ref[buffer, 0:64, g : g + 128] = high
-            both_ref[buffer, 64:128, g : g + 128] = low
-        columns_ref[m] = total
+    below = lax.broadcasted_iota(jnp.int32, (64 - slots, 128), 0)
+    padding = jnp.where(below == 0, 1.0, 0.0)
+
+    def chances(m, both_ref):
+        for b, units in enumerate(eights([m], draws)):
+            inverse_rows(units, b, columns_ref, raised_ref, parts_ref, inverse_ref)
+            for u, (_, g) in enumerate(units):
+                chance = raised_ref[m, :, g : g + 128] * columns_ref[m] * inverse_ref[b, u : u + 1, :]
+                padded = jnp.concatenate([chance, padding], axis=0)
+                high = padded.astype(jnp.bfloat16)
+                both_ref[0:64, g : g + 128] = high
+                both_ref[64:128, g : g + 128] = (padded - high.astype(jnp.float32)).astype(jnp.bfloat16)
+
+    def products(m, both_ref):
         product_ref[m] = lax.dot_general(
-            both_ref[buffer],
-            both_ref[buffer, 0:64, :],
-            (((1,), (1,)), ((), ())),
-            preferred_element_type=jnp.float32,
+            both_ref[...], both_ref[0:64, :], (((1,), (1,)), ((), ())), preferred_element_type=jnp.float32
         )
+
+    def pair(p, carry):
+        products(2 * p, even_ref)
+        chances(2 * p + 1, odd_ref)
+        products(2 * p + 1, odd_ref)
+        chances(2 * p + 2, even_ref)
+        return carry
+
+    chances(0, even_ref)
+    lax.fori_loop(0, own // 2 - 1, pair, 0)
+    products(own - 2, even_ref)
+    chances(own - 1, odd_ref)
+    products(own - 1, odd_ref)
     row = lax.broadcasted_iota(jnp.int32, (slots, slots), 0)
     col = lax.broadcasted_iota(jnp.int32, (slots, slots), 1)
     identity = jnp.where(row == col, 1.0, 0.0)
@@ -289,7 +320,7 @@
         product = product_ref[m]
         crossed = product[64:128]
         cross = (product[0:64] + crossed + jnp.transpose(crossed))[0:slots, 0:slots]
-        shares = jnp.sum(columns_ref[m], axis=1, keepdims=True)
+        shares = (product[0:64] + crossed)[0:slots, slots : slots + 1]
         valid = column(usable, m, slots) > 0.0
         paired = valid & (usable_rows[m : m + 1, 0:slots] > 0.0)
         divisor = jnp.where(valid, shares, 1.0)
@@ -306,6 +337,7 @@
     shape = lambda *sizes: jax.ShapeDtypeStruct(sizes, f32)
     state_shape = shape(5, slots, 8)
     columns = pltpu.VMEM((own, slots, 128), f32)
+    eight = [pltpu.VMEM((4, 64, 128), f32), pltpu.VMEM((4, 8, 128), f32)]
 
     def exchange(array, distance):
         return lax.ppermute(array, "draw", [(d, d ^ distance) for d in range(draw_count)])
@@ -330,6 +362,8 @@
             pltpu.VMEM((markets, slots, 6 * depth), bf16),
             pltpu.VMEM((markets, slots, span), f32),
             pltpu.VMEM((markets, slots, 128), f32),
+            pltpu.VMEM((markets, slots, 128), f32),
+            *eight,
             pltpu.SemaphoreType.DMA((8,)),
         ],
         compiler_params=params(),
@@ -369,7 +403,7 @@
         out_shape=(shape(own, slots, draws), state_shape, shape(every, 128)),
         in_specs=[VMEM] * 8,
         out_specs=(VMEM,) * 3,
-        scratch_shapes=[columns],
+        scratch_shapes=[columns, columns, *eight],
         compiler_params=params(),
         name="second",
     )(peaks, state, left, nu_near, partner, *received)
@@ -378,7 +412,7 @@
         out_shape=(state_shape, shape(draw_count, 16, 128)),
         in_specs=[VMEM] * 3,
         out_specs=(VMEM,) * 2,
-        scratch_shapes=[columns],
+        scratch_shapes=[columns, columns, *eight],
         compiler_params=params(),
         name="third",
     )(peaks_of(peak, EVERY), state, raised)
@@ -396,7 +430,7 @@
         out_shape=(shape(own, slots, slots), shape(markets, slots), shape(3)),
         in_specs=[VMEM] * 4,
         out_specs=(VMEM, VMEM, SMEM),
-        scratch_shapes=[pltpu.VMEM((2, 128, draws), bf16), columns, pltpu.VMEM((own, 128, 64), f32)],
+        scratch_shapes=[pltpu.VMEM((128, draws), bf16)] * 2 + [columns, pltpu.VMEM((own, 128, 64), f32), *eight],
         compiler_params=params(),
         name="final",
     )(peaks_of(peak, "mkt"), state, rows, raised)

time: 92.5 us -> 91.8 us (level)
  no operation moved by 1% of the time
where the time goes in v1:
time: 91.8 us; the launch traced here: 91.5 us
  blocking collectives  59.3 us (65%)
  Pallas kernels  12.8 us (14%)
  starting transfers between devices  11.3 us (12%)
  waiting for transfers between devices  7.29 us (8%)
    all_to_all x3, blocking collectives, peaks_of(): lax.all_to_all(peak.reshape(count, 1, 128), axis, 0, 0, tiled=True)  51.4 us
    all_to_all x1, blocking collectives, contract(): rows = lax.all_to_all(rows, 'draw', 0, 0, tiled=True)  7.95 us
    all_to_all x1, waiting for transfers between devices, contract(): sums = lax.all_to_all(sums, 'draw', 0, 0, tiled=True)  7.28 us
    ppermute x4, starting transfers between devices, exchange(): lax.ppermute(array, 'draw', [(d, d ^ distance) for d in range(draw_count)])  7.23 us
    pallas_call x1, Pallas kernels, contract(): pl.pallas_call(start_kernel, out_shape=(shape(3, slots, 128), shape(draw_...  4.51 us
    pallas_call x1, Pallas kernels, contract(): pl.pallas_call(final_kernel, out_shape=(shape(own, slots, slots), shape(m...  4.32 us
    all_to_all x1, starting transfers between devices, contract(): sums = lax.all_to_all(sums, 'draw', 0, 0, tiled=True)  4.11 us
    pallas_call x1, Pallas kernels, contract(): pl.pallas_call(second_kernel, out_shape=(shape(own, slots, draws), state_...  1.91 us
  transfers between devices with their start and end apart: 5, of which 1 were waited for; matrix products, arithmetic and copies ran while one was open for 0% of the time, Pallas kernels for 5%

profile of v1, /device:TPU:1, one launch (start us, length us, event | category | flops | bytes accessed | tf_op | source)
XLA Modules:
  0.0 91.5 jit_solution(16456006268643271271)
XLA Ops:
  0.6 3.3 %collective-permute-start = (f32[48,8,512]{2,1,0:T(8,128)}, f32[48,8,512]{2,1,0:T(8,128)S(1)}, u32[]{:S(2)}, u32[]{:S(2)}) collective-permute-start(f32[48,8,512]{2,1,0:T(8,128)} %nu_hbm.1), channel_id=1, source_target_pairs={{0,1},{1,0},{2,3},{3,2},{4,5},{5,4},{6,7},{7,6},{8,9},{9,8},{10,11... | collective-permute-start | bytes 2359304 | tf_op jit(solution)/shard_map/ppermute | solution.py:343
  3.9 4.5 %start.1 = (f32[3,56,128]{2,1,0:T(8,128)S(1)}, f32[8,32,128]{2,1,0:T(8,128)}, f32[48,8,512]{2,1,0:T(8,128)S(1)}, bf16[6,56,48]{2,1,0:T(8,128)(2,1)S(1)}) custom-call(s32[48]{0:T(128)} %counts_hbm.1, f32[8]{0:T(128)} %sigma_hbm.1, f32[48,56]{1,0:T(8,128)} %log_share_hbm.1, f32[48,8,56]{2,1,0:T(8,128)} %bitcast.19, f32[48,8,512]{2,1,0:T(8,128)} %nu_hbm.1), custom_call_target="tpu_custom_call" | custom-call | tf_op jit(solution)/shard_map/start/pallas_call | solution.py:351
  8.4 0.0 collective-permute-done.partner_ref
  8.5 0.1 collective-permute-start.1
  8.6 1.9 %collective-permute-start.2 = (f32[2,6,8,512]{3,2,1,0:T(8,128)S(1)}, f32[2,6,8,512]{3,2,1,0:T(8,128)S(1)}, u32[]{:S(2)}, u32[]{:S(2)}) collective-permute-start(f32[2,6,8,512]{3,2,1,0:T(8,128)S(1)} %get-tuple-element.27), channel_id=1, source_target_pairs={{0,4},{1,5},{2,6},{3,7},{4,0},{5,1},{6,2},{7,3},{8,12},{9,13},{10,... | collective-permute-start | bytes 589832 | tf_op jit(solution)/shard_map/ppermute | solution.py:343
  10.5 1.9 %collective-permute-start.3 = (f32[2,6,8,512]{3,2,1,0:T(8,128)S(1)}, f32[2,6,8,512]{3,2,1,0:T(8,128)S(1)}, u32[]{:S(2)}, u32[]{:S(2)}) collective-permute-start(f32[2,6,8,512]{3,2,1,0:T(8,128)S(1)} %get-tuple-element.28), channel_id=1, source_target_pairs={{0,6},{1,7},{2,4},{3,5},{4,2},{5,3},{6,0},{7,1},{8,14},{9,15},{10,... | collective-permute-start | bytes 589832 | tf_op jit(solution)/shard_map/ppermute | solution.py:343
  12.5 4.1 %all-to-all-start = ((f32[8,32,128]{2,1,0:T(8,128)}), f32[8,32,128]{2,1,0:T(8,128)S(1)}, u32[]{:S(2)}, u32[]{:S(2)}) async-start(f32[8,32,128]{2,1,0:T(8,128)} %get-tuple-element.20), calls=%async_computation | async-start | bytes 262144 | tf_op jit(solution)/shard_map/all_to_all | solution.py:383
  16.6 0.1 keep.1.refs_2_
  16.7 7.3 %all-to-all-done.refs_0_ = f32[8,32,128]{2,1,0:T(8,128)S(1)} async-done(((f32[8,32,128]{2,1,0:T(8,128)}), f32[8,32,128]{2,1,0:T(8,128)S(1)}, u32[]{:S(2)}, u32[]{:S(2)}) %all-to-all-start) | async-done | bytes 131104 | tf_op jit(solution)/shard_map/all_to_all | solution.py:383
  23.9 0.2 change.1
  24.2 19.6 %all_to_all.25 = f32[32,1,128]{2,1,0:T(1,128)S(1)} all-to-all(f32[32,1,128]{2,1,0:T(1,128)S(1)} %bitcast.18), channel_id=1, replica_groups=mesh['mkt'=32,'draw'=8] {'mkt'}, dimensions={0} | all-to-all | bytes 32768 | tf_op jit(solution)/shard_map/all_to_all | solution.py:347
  43.8 0.0 collective-permute-done.1.refs_0_
  43.8 0.0 collective-permute-done.2.refs_1_
  43.8 0.0 collective-permute-done.3.refs_2_
  43.8 1.9 %second.1 = (f32[6,56,4096]{2,1,0:T(8,128)S(1)}, f32[5,56,8]{2,1,0:T(8,128)S(1)}, f32[256,128]{1,0:T(8,128)S(1)}) custom-call(f32[32,128]{1,0:T(8,128)S(1)} %bitcast.15, f32[5,56,8]{2,1,0:T(8,128)S(1)} %get-tuple-element.23.state_ref, bf16[6,56,48]{2,1,0:T(8,128)(2,1)S(1)} %get-tuple-element.24.left_ref, f32[48,8,512]{2,1,0:T(8,128)S(1)} %get-tuple-element.25.nu_ref, ...), custom_call_target="tpu_custom_call" | custom-call | tf_op jit(solution)/shard_map/second/pallas_call | solution.py:401
  45.7 20.0 %all_to_all.26 = f32[256,1,128]{2,1,0:T(1,128)S(1)} all-to-all(f32[256,1,128]{2,1,0:T(1,128)S(1)} %bitcast.14), channel_id=1, replica_groups=mesh['mkt'=32,'draw'=8] {'mkt','draw'}, dimensions={0} | all-to-all | bytes 262144 | tf_op jit(solution)/shard_map/all_to_all | solution.py:347
  65.7 1.6 %third.1 = (f32[5,56,8]{2,1,0:T(8,128)S(1)}, f32[8,16,128]{2,1,0:T(8,128)S(1)}) custom-call(f32[256,128]{1,0:T(8,128)S(1)} %bitcast.13, f32[5,56,8]{2,1,0:T(8,128)S(1)} %get-tuple-element.30.state_ref, f32[6,56,4096]{2,1,0:T(8,128)S(1)} %get-tuple-element.31.raised_ref), custom_call_target="tpu_custom_call" | custom-call | tf_op jit(solution)/shard_map/third/pallas_call | solution.py:410
  67.3 7.9 %all_to_all.27.rows_ref = f32[8,16,128]{2,1,0:T(8,128)S(1)} all-to-all(f32[8,16,128]{2,1,0:T(8,128)S(1)} %get-tuple-element.32), channel_id=1, replica_groups=mesh['mkt'=32,'draw'=8] {'draw'}, dimensions={0} | all-to-all | bytes 131072 | tf_op jit(solution)/shard_map/all_to_all | solution.py:419
  75.3 0.1 join.1
  75.4 11.8 %all_to_all.28 = f32[32,1,128]{2,1,0:T(1,128)S(1)} all-to-all(f32[32,1,128]{2,1,0:T(1,128)S(1)} %bitcast.17), channel_id=1, replica_groups=mesh['mkt'=32,'draw'=8] {'mkt'}, dimensions={0} | all-to-all | bytes 32768 | tf_op jit(solution)/shard_map/all_to_all | solution.py:347
  87.1 4.3 %final.1 = (f32[6,56,56]{2,1,0:T(8,128)}, f32[48,56]{1,0:T(8,128)}, f32[3]{0:T(128)}) custom-call(f32[32,128]{1,0:T(8,128)S(1)} %bitcast.16, f32[5,56,8]{2,1,0:T(8,128)S(1)} %get-tuple-element.33.state_ref, f32[8,16,128]{2,1,0:T(8,128)S(1)} %all_to_all.27.rows_ref, f32[6,56,4096]{2,1,0:T(8,128)S(1)} %get-tuple-element.31.raised_ref), custom_call_target="tpu_custom_call" | custom-call | tf_op jit(solution)/shard_map/final/pallas_call | solution.py:428
  (1 shorter events, 0.0 us)
Async XLA Ops:
  0.6 7.8 %collective-permute-start = (f32[48,8,512]{2,1,0:T(8,128)}, f32[48,8,512]{2,1,0:T(8,128)S(1)}, u32[]{:S(2)}, u32[]{:S(2)}) collective-permute-start(f32[48,8,512]{2,1,0:T(8,128)} %nu_hbm.1), channel_id=1, source_target_pairs={{0,1},{1,0},{2,3},{3,2},{4,5},{5,4},{6,7},{7,6},{8,9},{9,8},{10,11... | collective-permute-start | bytes 2359304 | tf_op jit(solution)/shard_map/ppermute | solution.py:343
  8.5 35.3 %collective-permute-start.1 = (f32[2,6,8,512]{3,2,1,0:T(8,128)S(1)}, f32[2,6,8,512]{3,2,1,0:T(8,128)S(1)}, u32[]{:S(2)}, u32[]{:S(2)}) collective-permute-start(f32[2,6,8,512]{3,2,1,0:T(8,128)S(1)} %get-tuple-element.26), channel_id=1, source_target_pairs={{0,2},{1,3},{2,0},{3,1},{4,6},{5,7},{6,4},{7,5},{8,10},{9,11},{10,... | collective-permute-start | bytes 589832 | tf_op jit(solution)/shard_map/ppermute | solution.py:343
  8.6 35.2 %collective-permute-start.2 = (f32[2,6,8,512]{3,2,1,0:T(8,128)S(1)}, f32[2,6,8,512]{3,2,1,0:T(8,128)S(1)}, u32[]{:S(2)}, u32[]{:S(2)}) collective-permute-start(f32[2,6,8,512]{3,2,1,0:T(8,128)S(1)} %get-tuple-element.27), channel_id=1, source_target_pairs={{0,4},{1,5},{2,6},{3,7},{4,0},{5,1},{6,2},{7,3},{8,12},{9,13},{10,... | collective-permute-start | bytes 589832 | tf_op jit(solution)/shard_map/ppermute | solution.py:343
  10.5 33.2 %collective-permute-start.3 = (f32[2,6,8,512]{3,2,1,0:T(8,128)S(1)}, f32[2,6,8,512]{3,2,1,0:T(8,128)S(1)}, u32[]{:S(2)}, u32[]{:S(2)}) collective-permute-start(f32[2,6,8,512]{3,2,1,0:T(8,128)S(1)} %get-tuple-element.28), channel_id=1, source_target_pairs={{0,6},{1,7},{2,4},{3,5},{4,2},{5,3},{6,0},{7,1},{8,14},{9,15},{10,... | collective-permute-start | bytes 589832 | tf_op jit(solution)/shard_map/ppermute | solution.py:343
  12.5 11.5 %all-to-all-start = ((f32[8,32,128]{2,1,0:T(8,128)}), f32[8,32,128]{2,1,0:T(8,128)S(1)}, u32[]{:S(2)}, u32[]{:S(2)}) async-start(f32[8,32,128]{2,1,0:T(8,128)} %get-tuple-element.20), calls=%async_computation | async-start | bytes 262144 | tf_op jit(solution)/shard_map/all_to_all | solution.py:383

commit v2 on v1

--- a/solution.py
+++ b/solution.py
@@ -79,51 +79,46 @@
         columns_ref[m] = column(weights, m)
 
 
-def eights(markets, draws):
-    units = [(m, g) for m in markets for g in range(0, draws, 128)]
-    return [units[u : u + 8] for u in range(0, len(units), 8)]
-
-
-def inverse_rows(units, slot, columns_ref, raised_ref, parts_ref, inverse_ref):
-    slots = raised_ref.shape[1]
+def inverse_rows(columns_ref, raised_ref, parts_ref, inverse_ref):
+    markets, slots, draws = raised_ref.shape
+    units = [(m, g) for m in range(markets) for g in range(0, draws, 128)]
     for u, (m, g) in enumerate(units):
         part = raised_ref[m, 0:8, g : g + 128] * columns_ref[m, 0:8, :]
         for j in range(8, slots, 8):
             part = part + raised_ref[m, j : j + 8, g : g + 128] * columns_ref[m, j : j + 8, :]
-        parts_ref[slot, 8 * u : 8 * u + 8, :] = part
-    below = parts_ref[slot, pl.ds(0, 8, stride=8), :] + 1.0
-    for j in range(1, 8):
-        below = below + parts_ref[slot, pl.ds(j, 8, stride=8), :]
-    inverse_ref[slot] = 1.0 / below
+        parts_ref[8 * u : 8 * u + 8, :] = part
+    for u in range(0, len(units), 8):
+        below = parts_ref[pl.ds(8 * u, 8, stride=8), :] + 1.0
+        for j in range(1, 8):
+            below = below + parts_ref[pl.ds(8 * u + j, 8, stride=8), :]
+        inverse_ref[u : u + 8, :] = 1.0 / below
 
 
 def totals_over(columns_ref, raised_ref, parts_ref, inverse_ref, totals_ref):
     markets, slots, draws = raised_ref.shape
-    for b, units in enumerate(eights(range(markets), draws)):
-        slot = b % parts_ref.shape[0]
-        inverse_rows(units, slot, columns_ref, raised_ref, parts_ref, inverse_ref)
-        for m in sorted(set(m for m, _ in units)):
-            total = jnp.zeros((slots, 128), jnp.float32)
-            for u, (other, g) in enumerate(units):
-                if other == m:
-                    total = total + raised_ref[m, :, g : g + 128] * inverse_ref[slot, u : u + 1, :]
-            if any(g == 0 for other, g in units if other == m):
-                totals_ref[m] = total
-            else:
-                totals_ref[m] += total
-
-
-def packed_sums(totals_ref):
+    inverse_rows(columns_ref, raised_ref, parts_ref, inverse_ref)
+    groups = draws // 128
+    for m in range(markets):
+        total = jnp.zeros((slots, 128), jnp.float32)
+        for g in range(groups):
+            u = m * groups + g
+            total = total + raised_ref[m, :, 128 * g : 128 * g + 128] * inverse_ref[u : u + 1, :]
+        totals_ref[m] = total
+
+
+def send_lane_sums(sums_ref, totals_ref):
     markets, slots = totals_ref.shape[:2]
-    lane = lax.broadcasted_iota(jnp.int32, (32, 128), 1)
-    sums = jnp.zeros((32, 128), jnp.float32)
-    upper = jnp.zeros((32, 128), jnp.float32)
+    lane = lax.broadcasted_iota(jnp.int32, (slots, 128), 1)
+    ones = jnp.ones((256, 128), jnp.bfloat16)
+    sums = jnp.zeros((slots, 128), jnp.float32)
     for m in range(markets):
-        one = jnp.sum(totals_ref[m], axis=1, keepdims=True)
-        rest = jnp.concatenate([one[32:slots], jnp.zeros((64 - slots, 1), jnp.float32)], axis=0)
-        sums = jnp.where(lane == m, one[0:32], sums)
-        upper = jnp.where(lane == m + 64, rest, upper)
-    return jnp.where(lane < 64, sums, upper)
+        total = totals_ref[m]
+        high = total.astype(jnp.bfloat16)
+        low = (total - high.astype(jnp.float32)).astype(jnp.bfloat16)
+        both = jnp.concatenate([high, low], axis=1)
+        sums = jnp.where(lane == m, jnp.dot(both, ones, preferred_element_type=jnp.float32), sums)
+    rest = jnp.concatenate([sums[32:slots], jnp.zeros((64 - slots, 128), jnp.float32)], axis=0)
+    send_copies(sums_ref, jnp.where(lane[0:32] < 64, sums[0:32], pltpu.roll(rest, 64, axis=1)))
 
 
 def start_kernel(counts_hbm, sigma_hbm, log_share_hbm, x_hbm, nu_hbm, state_ref, sums_ref, nu_ref, kept_ref, counts_ref, sigma_ref, rows_ref, log_share_ref, x_ref, left_ref, raised_ref, columns_ref, totals_ref, parts_ref, inverse_ref, sems):
@@ -172,7 +167,7 @@
     for m in range(markets):
         raised_ref[m] = raise_tastes(left_ref[m], nu_ref[m])
     totals_over(columns_ref, raised_ref, parts_ref, inverse_ref, totals_ref)
-    send_copies(sums_ref, packed_sums(totals_ref))
+    send_lane_sums(sums_ref, totals_ref)
 
 
 def stage_kernel(nu_ref, partner_ref, *sends):
@@ -286,20 +281,27 @@
     below = lax.broadcasted_iota(jnp.int32, (64 - slots, 128), 0)
     padding = jnp.where(below == 0, 1.0, 0.0)
 
+    inverse_rows(columns_ref, raised_ref, parts_ref, inverse_ref)
+    groups = draws // 128
+
     def chances(m, both_ref):
-        for b, units in enumerate(eights([m], draws)):
-            inverse_rows(units, b, columns_ref, raised_ref, parts_ref, inverse_ref)
-            for u, (_, g) in enumerate(units):
-                chance = raised_ref[m, :, g : g + 128] * columns_ref[m] * inverse_ref[b, u : u + 1, :]
-                padded = jnp.concatenate([chance, padding], axis=0)
-                high = padded.astype(jnp.bfloat16)
-                both_ref[0:64, g : g + 128] = high
-                both_ref[64:128, g : g + 128] = (padded - high.astype(jnp.float32)).astype(jnp.bfloat16)
+        inverses = inverse_ref.at[pl.ds(m * groups, groups)]
+        for u in range(groups):
+            g = 128 * u
+            chance = raised_ref[m, :, g : g + 128] * columns_ref[m] * inverses[u : u + 1, :]
+            padded = jnp.concatenate([chance, padding], axis=0)
+            high = padded.astype(jnp.bfloat16)
+            both_ref[0:64, g : g + 128] = high
+            both_ref[64:128, g : g + 128] = (padded - high.astype(jnp.float32)).astype(jnp.bfloat16)
 
     def products(m, both_ref):
-        product_ref[m] = lax.dot_general(
-            both_ref[...], both_ref[0:64, :], (((1,), (1,)), ((), ())), preferred_element_type=jnp.float32
-        )
+        for half in (0, 64):
+            product_ref[m, half : half + 64, :] = lax.dot_general(
+                both_ref[half : half + 64, :],
+                both_ref[0:64, :],
+                (((1,), (1,)), ((), ())),
+                preferred_element_type=jnp.float32,
+            )
 
     def pair(p, carry):
         products(2 * p, even_ref)
@@ -337,7 +339,8 @@
     shape = lambda *sizes: jax.ShapeDtypeStruct(sizes, f32)
     state_shape = shape(5, slots, 8)
     columns = pltpu.VMEM((own, slots, 128), f32)
-    eight = [pltpu.VMEM((4, 64, 128), f32), pltpu.VMEM((4, 8, 128), f32)]
+    units = own * draws // 128
+    eight = [pltpu.VMEM((8 * units, 128), f32), pltpu.VMEM((units, 128), f32)]
 
     def exchange(array, distance):
         return lax.ppermute(array, "draw", [(d, d ^ distance) for d in range(draw_count)])

time: 91.8 us -> 91.3 us (level)
  no operation moved by 1% of the time
where the time goes in v2:
time: 91.3 us; the launch traced here: 90.9 us
  blocking collectives  59.4 us (65%)
  Pallas kernels  12.2 us (13%)
  starting transfers between devices  11.3 us (12%)
  waiting for transfers between devices  7.29 us (8%)
    all_to_all x3, blocking collectives, peaks_of(): lax.all_to_all(peak.reshape(count, 1, 128), axis, 0, 0, tiled=True)  51.4 us
    all_to_all x1, blocking collectives, contract(): rows = lax.all_to_all(rows, 'draw', 0, 0, tiled=True)  7.96 us
    all_to_all x1, waiting for transfers between devices, contract(): sums = lax.all_to_all(sums, 'draw', 0, 0, tiled=True)  7.28 us
    ppermute x4, starting transfers between devices, exchange(): lax.ppermute(array, 'draw', [(d, d ^ distance) for d in range(draw_count)])  7.23 us
    pallas_call x1, Pallas kernels, contract(): pl.pallas_call(start_kernel, out_shape=(shape(3, slots, 128), shape(draw_...  4.28 us
    all_to_all x1, starting transfers between devices, contract(): sums = lax.all_to_all(sums, 'draw', 0, 0, tiled=True)  4.12 us
    pallas_call x1, Pallas kernels, contract(): pl.pallas_call(final_kernel, out_shape=(shape(own, slots, slots), shape(m...  4.03 us
    pallas_call x1, Pallas kernels, contract(): pl.pallas_call(second_kernel, out_shape=(shape(own, slots, draws), state_...  2.01 us
  transfers between devices with their start and end apart: 5, of which 1 were waited for; matrix products, arithmetic and copies ran while one was open for 0% of the time, Pallas kernels for 5%

profile of v2, /device:TPU:1, one launch (start us, length us, event | category | flops | bytes accessed | tf_op | source)
XLA Modules:
  0.0 90.9 jit_solution(9602388138037564610)
XLA Ops:
  0.6 3.3 %collective-permute-start = (f32[48,8,512]{2,1,0:T(8,128)}, f32[48,8,512]{2,1,0:T(8,128)S(1)}, u32[]{:S(2)}, u32[]{:S(2)}) collective-permute-start(f32[48,8,512]{2,1,0:T(8,128)} %nu_hbm.1), channel_id=1, source_target_pairs={{0,1},{1,0},{2,3},{3,2},{4,5},{5,4},{6,7},{7,6},{8,9},{9,8},{10,11... | collective-permute-start | bytes 2359304 | tf_op jit(solution)/shard_map/ppermute | solution.py:346
  3.9 4.3 %start.1 = (f32[3,56,128]{2,1,0:T(8,128)S(1)}, f32[8,32,128]{2,1,0:T(8,128)}, f32[48,8,512]{2,1,0:T(8,128)S(1)}, bf16[6,56,48]{2,1,0:T(8,128)(2,1)S(1)}) custom-call(s32[48]{0:T(128)} %counts_hbm.1, f32[8]{0:T(128)} %sigma_hbm.1, f32[48,56]{1,0:T(8,128)} %log_share_hbm.1, f32[48,8,56]{2,1,0:T(8,128)} %bitcast.19, f32[48,8,512]{2,1,0:T(8,128)} %nu_hbm.1), custom_call_target="tpu_custom_call" | custom-call | tf_op jit(solution)/shard_map/start/pallas_call | solution.py:354
  8.2 0.0 collective-permute-done.partner_ref
  8.3 0.1 collective-permute-start.1
  8.4 1.9 %collective-permute-start.2 = (f32[2,6,8,512]{3,2,1,0:T(8,128)S(1)}, f32[2,6,8,512]{3,2,1,0:T(8,128)S(1)}, u32[]{:S(2)}, u32[]{:S(2)}) collective-permute-start(f32[2,6,8,512]{3,2,1,0:T(8,128)S(1)} %get-tuple-element.27), channel_id=1, source_target_pairs={{0,4},{1,5},{2,6},{3,7},{4,0},{5,1},{6,2},{7,3},{8,12},{9,13},{10,... | collective-permute-start | bytes 589832 | tf_op jit(solution)/shard_map/ppermute | solution.py:346
  10.3 1.9 %collective-permute-start.3 = (f32[2,6,8,512]{3,2,1,0:T(8,128)S(1)}, f32[2,6,8,512]{3,2,1,0:T(8,128)S(1)}, u32[]{:S(2)}, u32[]{:S(2)}) collective-permute-start(f32[2,6,8,512]{3,2,1,0:T(8,128)S(1)} %get-tuple-element.28), channel_id=1, source_target_pairs={{0,6},{1,7},{2,4},{3,5},{4,2},{5,3},{6,0},{7,1},{8,14},{9,15},{10,... | collective-permute-start | bytes 589832 | tf_op jit(solution)/shard_map/ppermute | solution.py:346
  12.2 4.1 %all-to-all-start = ((f32[8,32,128]{2,1,0:T(8,128)}), f32[8,32,128]{2,1,0:T(8,128)S(1)}, u32[]{:S(2)}, u32[]{:S(2)}) async-start(f32[8,32,128]{2,1,0:T(8,128)} %get-tuple-element.20), calls=%async_computation | async-start | bytes 262144 | tf_op jit(solution)/shard_map/all_to_all | solution.py:386
  16.3 0.1 keep.1.refs_2_
  16.4 7.3 %all-to-all-done.refs_0_ = f32[8,32,128]{2,1,0:T(8,128)S(1)} async-done(((f32[8,32,128]{2,1,0:T(8,128)}), f32[8,32,128]{2,1,0:T(8,128)S(1)}, u32[]{:S(2)}, u32[]{:S(2)}) %all-to-all-start) | async-done | bytes 131104 | tf_op jit(solution)/shard_map/all_to_all | solution.py:386
  23.7 0.2 change.1
  23.9 19.6 %all_to_all.25 = f32[32,1,128]{2,1,0:T(1,128)S(1)} all-to-all(f32[32,1,128]{2,1,0:T(1,128)S(1)} %bitcast.18), channel_id=1, replica_groups=mesh['mkt'=32,'draw'=8] {'mkt'}, dimensions={0} | all-to-all | bytes 32768 | tf_op jit(solution)/shard_map/all_to_all | solution.py:350
  43.6 0.0 collective-permute-done.1.refs_0_
  43.6 0.0 collective-permute-done.2.refs_1_
  43.6 0.0 collective-permute-done.3.refs_2_
  43.6 2.0 %second.1 = (f32[6,56,4096]{2,1,0:T(8,128)S(1)}, f32[5,56,8]{2,1,0:T(8,128)S(1)}, f32[256,128]{1,0:T(8,128)S(1)}) custom-call(f32[32,128]{1,0:T(8,128)S(1)} %bitcast.15, f32[5,56,8]{2,1,0:T(8,128)S(1)} %get-tuple-element.23.state_ref, bf16[6,56,48]{2,1,0:T(8,128)(2,1)S(1)} %get-tuple-element.24.left_ref, f32[48,8,512]{2,1,0:T(8,128)S(1)} %get-tuple-element.25.nu_ref, ...), custom_call_target="tpu_custom_call" | custom-call | tf_op jit(solution)/shard_map/second/pallas_call | solution.py:404
  45.6 20.0 %all_to_all.26 = f32[256,1,128]{2,1,0:T(1,128)S(1)} all-to-all(f32[256,1,128]{2,1,0:T(1,128)S(1)} %bitcast.14), channel_id=1, replica_groups=mesh['mkt'=32,'draw'=8] {'mkt','draw'}, dimensions={0} | all-to-all | bytes 262144 | tf_op jit(solution)/shard_map/all_to_all | solution.py:350
  65.6 1.4 %third.1 = (f32[5,56,8]{2,1,0:T(8,128)S(1)}, f32[8,16,128]{2,1,0:T(8,128)S(1)}) custom-call(f32[256,128]{1,0:T(8,128)S(1)} %bitcast.13, f32[5,56,8]{2,1,0:T(8,128)S(1)} %get-tuple-element.30.state_ref, f32[6,56,4096]{2,1,0:T(8,128)S(1)} %get-tuple-element.31.raised_ref), custom_call_target="tpu_custom_call" | custom-call | tf_op jit(solution)/shard_map/third/pallas_call | solution.py:413
  67.0 8.0 %all_to_all.27.rows_ref = f32[8,16,128]{2,1,0:T(8,128)S(1)} all-to-all(f32[8,16,128]{2,1,0:T(8,128)S(1)} %get-tuple-element.32), channel_id=1, replica_groups=mesh['mkt'=32,'draw'=8] {'draw'}, dimensions={0} | all-to-all | bytes 131072 | tf_op jit(solution)/shard_map/all_to_all | solution.py:422
  75.0 0.1 join.1
  75.1 11.8 %all_to_all.28 = f32[32,1,128]{2,1,0:T(1,128)S(1)} all-to-all(f32[32,1,128]{2,1,0:T(1,128)S(1)} %bitcast.17), channel_id=1, replica_groups=mesh['mkt'=32,'draw'=8] {'mkt'}, dimensions={0} | all-to-all | bytes 32768 | tf_op jit(solution)/shard_map/all_to_all | solution.py:350
  86.9 4.0 %final.1 = (f32[6,56,56]{2,1,0:T(8,128)}, f32[48,56]{1,0:T(8,128)}, f32[3]{0:T(128)}) custom-call(f32[32,128]{1,0:T(8,128)S(1)} %bitcast.16, f32[5,56,8]{2,1,0:T(8,128)S(1)} %get-tuple-element.33.state_ref, f32[8,16,128]{2,1,0:T(8,128)S(1)} %all_to_all.27.rows_ref, f32[6,56,4096]{2,1,0:T(8,128)S(1)} %get-tuple-element.31.raised_ref), custom_call_target="tpu_custom_call" | custom-call | tf_op jit(solution)/shard_map/final/pallas_call | solution.py:431
  (1 shorter events, 0.0 us)
Async XLA Ops:
  0.6 7.6 %collective-permute-start = (f32[48,8,512]{2,1,0:T(8,128)}, f32[48,8,512]{2,1,0:T(8,128)S(1)}, u32[]{:S(2)}, u32[]{:S(2)}) collective-permute-start(f32[48,8,512]{2,1,0:T(8,128)} %nu_hbm.1), channel_id=1, source_target_pairs={{0,1},{1,0},{2,3},{3,2},{4,5},{5,4},{6,7},{7,6},{8,9},{9,8},{10,11... | collective-permute-start | bytes 2359304 | tf_op jit(solution)/shard_map/ppermute | solution.py:346
  8.3 35.3 %collective-permute-start.1 = (f32[2,6,8,512]{3,2,1,0:T(8,128)S(1)}, f32[2,6,8,512]{3,2,1,0:T(8,128)S(1)}, u32[]{:S(2)}, u32[]{:S(2)}) collective-permute-start(f32[2,6,8,512]{3,2,1,0:T(8,128)S(1)} %get-tuple-element.26), channel_id=1, source_target_pairs={{0,2},{1,3},{2,0},{3,1},{4,6},{5,7},{6,4},{7,5},{8,10},{9,11},{10,... | collective-permute-start | bytes 589832 | tf_op jit(solution)/shard_map/ppermute | solution.py:346
  8.4 35.2 %collective-permute-start.2 = (f32[2,6,8,512]{3,2,1,0:T(8,128)S(1)}, f32[2,6,8,512]{3,2,1,0:T(8,128)S(1)}, u32[]{:S(2)}, u32[]{:S(2)}) collective-permute-start(f32[2,6,8,512]{3,2,1,0:T(8,128)S(1)} %get-tuple-element.27), channel_id=1, source_target_pairs={{0,4},{1,5},{2,6},{3,7},{4,0},{5,1},{6,2},{7,3},{8,12},{9,13},{10,... | collective-permute-start | bytes 589832 | tf_op jit(solution)/shard_map/ppermute | solution.py:346
  10.3 33.2 %collective-permute-start.3 = (f32[2,6,8,512]{3,2,1,0:T(8,128)S(1)}, f32[2,6,8,512]{3,2,1,0:T(8,128)S(1)}, u32[]{:S(2)}, u32[]{:S(2)}) collective-permute-start(f32[2,6,8,512]{3,2,1,0:T(8,128)S(1)} %get-tuple-element.28), channel_id=1, source_target_pairs={{0,6},{1,7},{2,4},{3,5},{4,2},{5,3},{6,0},{7,1},{8,14},{9,15},{10,... | collective-permute-start | bytes 589832 | tf_op jit(solution)/shard_map/ppermute | solution.py:346
  12.2 11.5 %all-to-all-start = ((f32[8,32,128]{2,1,0:T(8,128)}), f32[8,32,128]{2,1,0:T(8,128)S(1)}, u32[]{:S(2)}, u32[]{:S(2)}) async-start(f32[8,32,128]{2,1,0:T(8,128)} %get-tuple-element.20), calls=%async_computation | async-start | bytes 262144 | tf_op jit(solution)/shard_map/all_to_all | solution.py:386

commit v3 on v2

--- a/solution.py
+++ b/solution.py
@@ -34,7 +34,8 @@
 
 
 def fill(ref, value):
-    tile = jnp.broadcast_to(value, (8, ref.shape[1]))
+    largest = jnp.max(jnp.max(jnp.abs(value), axis=0, keepdims=True), axis=1, keepdims=True)
+    tile = jnp.broadcast_to(largest, (8, ref.shape[1]))
     for row in range(0, ref.shape[0], 8):
         ref[row : row + 8, :] = tile
 
@@ -198,7 +199,7 @@
     usable = all_ref[1] > 0.0
     shares = sums * usable_weights(all_ref, all_ref[2]) * inverse
     change = jnp.where(usable, all_ref[0] - jnp.log(jnp.where(usable, shares, 1.0)), 0.0)
-    fill(peak_ref, jnp.max(jnp.abs(change)))
+    fill(peak_ref, change)
     kept = lax.broadcasted_iota(jnp.int32, (slots, 8), 1) < own
     for p in range(3):
         state_ref[p] = kept_ref[p]
@@ -207,10 +208,12 @@
 
 
 def moved(turn, peaks_ref, state_ref):
-    largest = jnp.max(peaks_ref[...])
+    largest = jnp.max(peaks_ref[...], axis=0, keepdims=True)
     step = jnp.minimum(1.0, step_cap / (largest + epsilon))
     row = lax.broadcasted_iota(jnp.int32, state_ref.shape[1:], 0)
-    return step, state_ref[2] + step * state_ref[3], jnp.where(row == turn, largest, state_ref[4])
+    width = state_ref.shape[2]
+    norms = jnp.where(row == turn, largest[:, 0:width], state_ref[4])
+    return step, state_ref[2] + step[:, 0:width] * state_ref[3], norms
 
 
 def next_change(turn, peaks_ref, state_ref, out_ref, raised_ref, columns_ref, totals_ref, *eight):
@@ -247,7 +250,7 @@
         for s, source in enumerate(sources):
             raised_ref[m, :, s * span : (s + 1) * span] = raise_tastes(left_ref[m], source[m])
     _, change = next_change(0, peaks_ref, state_ref, out_ref, raised_ref, *scratch)
-    fill(peak_ref, jnp.max(jnp.abs(change)))
+    fill(peak_ref, change)
 
 
 def as_rows(value):
@@ -264,10 +267,10 @@
     largest = jnp.abs(rows_ref[0, 8:16, :])
     for d in range(1, rows_ref.shape[0]):
         largest = jnp.maximum(largest, jnp.abs(rows_ref[d, 8:16, :]))
-    fill(peak_ref, jnp.max(largest))
-
-
-def final_kernel(peaks_ref, state_ref, rows_ref, raised_ref, jacobian_ref, mean_ref, norms_ref, even_ref, odd_ref, columns_ref, product_ref, parts_ref, inverse_ref):
+    fill(peak_ref, largest)
+
+
+def final_kernel(peaks_ref, state_ref, rows_ref, raised_ref, jacobian_hbm, mean_hbm, norms_ref, jacobian_ref, mean_ref, sems, even_ref, odd_ref, columns_ref, product_ref, parts_ref, inverse_ref):
     own, slots, draws = raised_ref.shape
     step, mean_util, norms = moved(2, peaks_ref, state_ref)
     usable = state_ref[1]
@@ -278,6 +281,7 @@
     for d in range(rows_ref.shape[0]):
         rows = rows_ref[d, 0:8, :] + step * rows_ref[d, 8:16, :]
         mean_ref[d * own : (d + 1) * own, :] = rows[0:own, 0:slots]
+    copies = both_starts([pltpu.make_async_copy(mean_ref, mean_hbm, sems.at[own])])
     below = lax.broadcasted_iota(jnp.int32, (64 - slots, 128), 0)
     padding = jnp.where(below == 0, 1.0, 0.0)
 
@@ -327,6 +331,9 @@
         paired = valid & (usable_rows[m : m + 1, 0:slots] > 0.0)
         divisor = jnp.where(valid, shares, 1.0)
         jacobian_ref[m] = jnp.where(paired, identity - cross / divisor, 0.0)
+        copies += both_starts([pltpu.make_async_copy(jacobian_ref.at[m], jacobian_hbm.at[m], sems.at[m])])
+    for copy in copies:
+        copy.wait()
 
 
 def contract(x_char, nu_draws, coef_sigma, log_share, counts):
@@ -432,8 +439,13 @@
         final_kernel,
         out_shape=(shape(own, slots, slots), shape(markets, slots), shape(3)),
         in_specs=[VMEM] * 4,
-        out_specs=(VMEM, VMEM, SMEM),
-        scratch_shapes=[pltpu.VMEM((128, draws), bf16)] * 2 + [columns, pltpu.VMEM((own, 128, 64), f32), *eight],
+        out_specs=(HBM, HBM, SMEM),
+        scratch_shapes=[
+            pltpu.VMEM((own, slots, slots), f32),
+            pltpu.VMEM((markets, slots), f32),
+            pltpu.SemaphoreType.DMA((own + 1,)),
+        ]
+        + [pltpu.VMEM((128, draws), bf16)] * 2 + [columns, pltpu.VMEM((own, 128, 64), f32), *eight],
         compiler_params=params(),
         name="final",
     )(peaks_of(peak, "mkt"), state, rows, raised)

time: 91.3 us -> 91.3 us (level)
  no operation moved by 1% of the time
where the time goes in v3:
time: 91.3 us; the launch traced here: 90.9 us
  blocking collectives  59.3 us (65%)
  Pallas kernels  12.3 us (13%)
  starting transfers between devices  11.3 us (12%)
  waiting for transfers between devices  7.29 us (8%)
    all_to_all x3, blocking collectives, peaks_of(): lax.all_to_all(peak.reshape(count, 1, 128), axis, 0, 0, tiled=True)  51.4 us
    all_to_all x1, blocking collectives, contract(): rows = lax.all_to_all(rows, 'draw', 0, 0, tiled=True)  7.95 us
    all_to_all x1, waiting for transfers between devices, contract(): sums = lax.all_to_all(sums, 'draw', 0, 0, tiled=True)  7.28 us
    ppermute x4, starting transfers between devices, exchange(): lax.ppermute(array, 'draw', [(d, d ^ distance) for d in range(draw_count)])  7.23 us
    pallas_call x1, Pallas kernels, contract(): pl.pallas_call(final_kernel, out_shape=(shape(own, slots, slots), shape(m...  4.41 us
    pallas_call x1, Pallas kernels, contract(): pl.pallas_call(start_kernel, out_shape=(shape(3, slots, 128), shape(draw_...  4.28 us
    all_to_all x1, starting transfers between devices, contract(): sums = lax.all_to_all(sums, 'draw', 0, 0, tiled=True)  4.12 us
    pallas_call x1, Pallas kernels, contract(): pl.pallas_call(second_kernel, out_shape=(shape(own, slots, draws), state_...  1.89 us
  transfers between devices with their start and end apart: 5, of which 1 were waited for; matrix products, arithmetic and copies ran while one was open for 0% of the time, Pallas kernels for 5%

profile of v3, /device:TPU:1, one launch (start us, length us, event | category | flops | bytes accessed | tf_op | source)
XLA Modules:
  0.0 90.9 jit_solution(5390719722251995864)
XLA Ops:
  0.6 3.3 %collective-permute-start = (f32[48,8,512]{2,1,0:T(8,128)}, f32[48,8,512]{2,1,0:T(8,128)S(1)}, u32[]{:S(2)}, u32[]{:S(2)}) collective-permute-start(f32[48,8,512]{2,1,0:T(8,128)} %nu_hbm.1), channel_id=1, source_target_pairs={{0,1},{1,0},{2,3},{3,2},{4,5},{5,4},{6,7},{7,6},{8,9},{9,8},{10,11... | collective-permute-start | bytes 2359304 | tf_op jit(solution)/shard_map/ppermute | solution.py:353
  3.9 4.3 %start.1 = (f32[3,56,128]{2,1,0:T(8,128)S(1)}, f32[8,32,128]{2,1,0:T(8,128)}, f32[48,8,512]{2,1,0:T(8,128)S(1)}, bf16[6,56,48]{2,1,0:T(8,128)(2,1)S(1)}) custom-call(s32[48]{0:T(128)} %counts_hbm.1, f32[8]{0:T(128)} %sigma_hbm.1, f32[48,56]{1,0:T(8,128)} %log_share_hbm.1, f32[48,8,56]{2,1,0:T(8,128)} %bitcast.19, f32[48,8,512]{2,1,0:T(8,128)} %nu_hbm.1), custom_call_target="tpu_custom_call" | custom-call | tf_op jit(solution)/shard_map/start/pallas_call | solution.py:361
  8.2 0.0 collective-permute-done.partner_ref
  8.3 0.1 collective-permute-start.1
  8.4 1.9 %collective-permute-start.2 = (f32[2,6,8,512]{3,2,1,0:T(8,128)S(1)}, f32[2,6,8,512]{3,2,1,0:T(8,128)S(1)}, u32[]{:S(2)}, u32[]{:S(2)}) collective-permute-start(f32[2,6,8,512]{3,2,1,0:T(8,128)S(1)} %get-tuple-element.27), channel_id=1, source_target_pairs={{0,4},{1,5},{2,6},{3,7},{4,0},{5,1},{6,2},{7,3},{8,12},{9,13},{10,... | collective-permute-start | bytes 589832 | tf_op jit(solution)/shard_map/ppermute | solution.py:353
  10.3 1.9 %collective-permute-start.3 = (f32[2,6,8,512]{3,2,1,0:T(8,128)S(1)}, f32[2,6,8,512]{3,2,1,0:T(8,128)S(1)}, u32[]{:S(2)}, u32[]{:S(2)}) collective-permute-start(f32[2,6,8,512]{3,2,1,0:T(8,128)S(1)} %get-tuple-element.28), channel_id=1, source_target_pairs={{0,6},{1,7},{2,4},{3,5},{4,2},{5,3},{6,0},{7,1},{8,14},{9,15},{10,... | collective-permute-start | bytes 589832 | tf_op jit(solution)/shard_map/ppermute | solution.py:353
  12.2 4.1 %all-to-all-start = ((f32[8,32,128]{2,1,0:T(8,128)}), f32[8,32,128]{2,1,0:T(8,128)S(1)}, u32[]{:S(2)}, u32[]{:S(2)}) async-start(f32[8,32,128]{2,1,0:T(8,128)} %get-tuple-element.20), calls=%async_computation | async-start | bytes 262144 | tf_op jit(solution)/shard_map/all_to_all | solution.py:393
  16.3 0.1 keep.1.refs_2_
  16.4 7.3 %all-to-all-done.refs_0_ = f32[8,32,128]{2,1,0:T(8,128)S(1)} async-done(((f32[8,32,128]{2,1,0:T(8,128)}), f32[8,32,128]{2,1,0:T(8,128)S(1)}, u32[]{:S(2)}, u32[]{:S(2)}) %all-to-all-start) | async-done | bytes 131104 | tf_op jit(solution)/shard_map/all_to_all | solution.py:393
  23.7 0.2 change.1
  23.9 19.6 %all_to_all.25 = f32[32,1,128]{2,1,0:T(1,128)S(1)} all-to-all(f32[32,1,128]{2,1,0:T(1,128)S(1)} %bitcast.18), channel_id=1, replica_groups=mesh['mkt'=32,'draw'=8] {'mkt'}, dimensions={0} | all-to-all | bytes 32768 | tf_op jit(solution)/shard_map/all_to_all | solution.py:357
  43.5 0.0 collective-permute-done.1.refs_0_
  43.5 0.0 collective-permute-done.2.refs_1_
  43.5 0.0 collective-permute-done.3.refs_2_
  43.5 1.9 %second.1 = (f32[6,56,4096]{2,1,0:T(8,128)S(1)}, f32[5,56,8]{2,1,0:T(8,128)S(1)}, f32[256,128]{1,0:T(8,128)S(1)}) custom-call(f32[32,128]{1,0:T(8,128)S(1)} %bitcast.15, f32[5,56,8]{2,1,0:T(8,128)S(1)} %get-tuple-element.23.state_ref, bf16[6,56,48]{2,1,0:T(8,128)(2,1)S(1)} %get-tuple-element.24.left_ref, f32[48,8,512]{2,1,0:T(8,128)S(1)} %get-tuple-element.25.nu_ref, ...), custom_call_target="tpu_custom_call" | custom-call | tf_op jit(solution)/shard_map/second/pallas_call | solution.py:411
  45.4 20.0 %all_to_all.26 = f32[256,1,128]{2,1,0:T(1,128)S(1)} all-to-all(f32[256,1,128]{2,1,0:T(1,128)S(1)} %bitcast.14), channel_id=1, replica_groups=mesh['mkt'=32,'draw'=8] {'mkt','draw'}, dimensions={0} | all-to-all | bytes 262144 | tf_op jit(solution)/shard_map/all_to_all | solution.py:357
  65.4 1.3 %third.1 = (f32[5,56,8]{2,1,0:T(8,128)S(1)}, f32[8,16,128]{2,1,0:T(8,128)S(1)}) custom-call(f32[256,128]{1,0:T(8,128)S(1)} %bitcast.13, f32[5,56,8]{2,1,0:T(8,128)S(1)} %get-tuple-element.30.state_ref, f32[6,56,4096]{2,1,0:T(8,128)S(1)} %get-tuple-element.31.raised_ref), custom_call_target="tpu_custom_call" | custom-call | tf_op jit(solution)/shard_map/third/pallas_call | solution.py:420
  66.8 7.9 %all_to_all.27.rows_ref = f32[8,16,128]{2,1,0:T(8,128)S(1)} all-to-all(f32[8,16,128]{2,1,0:T(8,128)S(1)} %get-tuple-element.32), channel_id=1, replica_groups=mesh['mkt'=32,'draw'=8] {'draw'}, dimensions={0} | all-to-all | bytes 131072 | tf_op jit(solution)/shard_map/all_to_all | solution.py:429
  74.7 0.1 join.1
  74.8 11.7 %all_to_all.28 = f32[32,1,128]{2,1,0:T(1,128)S(1)} all-to-all(f32[32,1,128]{2,1,0:T(1,128)S(1)} %bitcast.17), channel_id=1, replica_groups=mesh['mkt'=32,'draw'=8] {'mkt'}, dimensions={0} | all-to-all | bytes 32768 | tf_op jit(solution)/shard_map/all_to_all | solution.py:357
  86.5 4.4 %final.1 = (f32[6,56,56]{2,1,0:T(8,128)}, f32[48,56]{1,0:T(8,128)}, f32[3]{0:T(128)}) custom-call(f32[32,128]{1,0:T(8,128)S(1)} %bitcast.16, f32[5,56,8]{2,1,0:T(8,128)S(1)} %get-tuple-element.33.state_ref, f32[8,16,128]{2,1,0:T(8,128)S(1)} %all_to_all.27.rows_ref, f32[6,56,4096]{2,1,0:T(8,128)S(1)} %get-tuple-element.31.raised_ref), custom_call_target="tpu_custom_call" | custom-call | tf_op jit(solution)/shard_map/final/pallas_call | solution.py:438
  (1 shorter events, 0.0 us)
Async XLA Ops:
  0.6 7.6 %collective-permute-start = (f32[48,8,512]{2,1,0:T(8,128)}, f32[48,8,512]{2,1,0:T(8,128)S(1)}, u32[]{:S(2)}, u32[]{:S(2)}) collective-permute-start(f32[48,8,512]{2,1,0:T(8,128)} %nu_hbm.1), channel_id=1, source_target_pairs={{0,1},{1,0},{2,3},{3,2},{4,5},{5,4},{6,7},{7,6},{8,9},{9,8},{10,11... | collective-permute-start | bytes 2359304 | tf_op jit(solution)/shard_map/ppermute | solution.py:353
  8.3 35.2 %collective-permute-start.1 = (f32[2,6,8,512]{3,2,1,0:T(8,128)S(1)}, f32[2,6,8,512]{3,2,1,0:T(8,128)S(1)}, u32[]{:S(2)}, u32[]{:S(2)}) collective-permute-start(f32[2,6,8,512]{3,2,1,0:T(8,128)S(1)} %get-tuple-element.26), channel_id=1, source_target_pairs={{0,2},{1,3},{2,0},{3,1},{4,6},{5,7},{6,4},{7,5},{8,10},{9,11},{10,... | collective-permute-start | bytes 589832 | tf_op jit(solution)/shard_map/ppermute | solution.py:353
  8.4 35.1 %collective-permute-start.2 = (f32[2,6,8,512]{3,2,1,0:T(8,128)S(1)}, f32[2,6,8,512]{3,2,1,0:T(8,128)S(1)}, u32[]{:S(2)}, u32[]{:S(2)}) collective-permute-start(f32[2,6,8,512]{3,2,1,0:T(8,128)S(1)} %get-tuple-element.27), channel_id=1, source_target_pairs={{0,4},{1,5},{2,6},{3,7},{4,0},{5,1},{6,2},{7,3},{8,12},{9,13},{10,... | collective-permute-start | bytes 589832 | tf_op jit(solution)/shard_map/ppermute | solution.py:353
  10.3 33.2 %collective-permute-start.3 = (f32[2,6,8,512]{3,2,1,0:T(8,128)S(1)}, f32[2,6,8,512]{3,2,1,0:T(8,128)S(1)}, u32[]{:S(2)}, u32[]{:S(2)}) collective-permute-start(f32[2,6,8,512]{3,2,1,0:T(8,128)S(1)} %get-tuple-element.28), channel_id=1, source_target_pairs={{0,6},{1,7},{2,4},{3,5},{4,2},{5,3},{6,0},{7,1},{8,14},{9,15},{10,... | collective-permute-start | bytes 589832 | tf_op jit(solution)/shard_map/ppermute | solution.py:353
  12.2 11.5 %all-to-all-start = ((f32[8,32,128]{2,1,0:T(8,128)}), f32[8,32,128]{2,1,0:T(8,128)S(1)}, u32[]{:S(2)}, u32[]{:S(2)}) async-start(f32[8,32,128]{2,1,0:T(8,128)} %get-tuple-element.20), calls=%async_computation | async-start | bytes 262144 | tf_op jit(solution)/shard_map/all_to_all | solution.py:393

commit v4 on v3

--- a/solution.py
+++ b/solution.py
@@ -270,7 +270,7 @@
     fill(peak_ref, largest)
 
 
-def final_kernel(peaks_ref, state_ref, rows_ref, raised_ref, jacobian_hbm, mean_hbm, norms_ref, jacobian_ref, mean_ref, sems, even_ref, odd_ref, columns_ref, product_ref, parts_ref, inverse_ref):
+def final_kernel(peaks_ref, state_ref, rows_ref, raised_ref, jacobian_ref, mean_ref, norms_ref, even_ref, odd_ref, columns_ref, product_ref, parts_ref, inverse_ref):
     own, slots, draws = raised_ref.shape
     step, mean_util, norms = moved(2, peaks_ref, state_ref)
     usable = state_ref[1]
@@ -281,7 +281,6 @@
     for d in range(rows_ref.shape[0]):
         rows = rows_ref[d, 0:8, :] + step * rows_ref[d, 8:16, :]
         mean_ref[d * own : (d + 1) * own, :] = rows[0:own, 0:slots]
-    copies = both_starts([pltpu.make_async_copy(mean_ref, mean_hbm, sems.at[own])])
     below = lax.broadcasted_iota(jnp.int32, (64 - slots, 128), 0)
     padding = jnp.where(below == 0, 1.0, 0.0)
 
@@ -331,9 +330,6 @@
         paired = valid & (usable_rows[m : m + 1, 0:slots] > 0.0)
         divisor = jnp.where(valid, shares, 1.0)
         jacobian_ref[m] = jnp.where(paired, identity - cross / divisor, 0.0)
-        copies += both_starts([pltpu.make_async_copy(jacobian_ref.at[m], jacobian_hbm.at[m], sems.at[m])])
-    for copy in copies:
-        copy.wait()
 
 
 def contract(x_char, nu_draws, coef_sigma, log_share, counts):
@@ -347,7 +343,7 @@
     state_shape = shape(5, slots, 8)
     columns = pltpu.VMEM((own, slots, 128), f32)
     units = own * draws // 128
-    eight = [pltpu.VMEM((8 * units, 128), f32), pltpu.VMEM((units, 128), f32)]
+    eight = [pltpu.VMEM((8 * units + 64, 128), f32), pltpu.VMEM((units, 128), f32)]
 
     def exchange(array, distance):
         return lax.ppermute(array, "draw", [(d, d ^ distance) for d in range(draw_count)])
@@ -439,13 +435,8 @@
         final_kernel,
         out_shape=(shape(own, slots, slots), shape(markets, slots), shape(3)),
         in_specs=[VMEM] * 4,
-        out_specs=(HBM, HBM, SMEM),
-        scratch_shapes=[
-            pltpu.VMEM((own, slots, slots), f32),
-            pltpu.VMEM((markets, slots), f32),
-            pltpu.SemaphoreType.DMA((own + 1,)),
-        ]
-        + [pltpu.VMEM((128, draws), bf16)] * 2 + [columns, pltpu.VMEM((own, 128, 64), f32), *eight],
+        out_specs=(VMEM, VMEM, SMEM),
+        scratch_shapes=[pltpu.VMEM((128, draws), bf16)] * 2 + [columns, pltpu.VMEM((own, 128, 64), f32), *eight],
         compiler_params=params(),
         name="final",
     )(peaks_of(peak, "mkt"), state, rows, raised)

time: 91.3 us -> 90.8 us (level)
  no operation moved by 1% of the time
where the time goes in v4:
time: 90.8 us; the launch traced here: 90.4 us
  blocking collectives  59.3 us (65%)
  Pallas kernels  11.8 us (13%)
  starting transfers between devices  11.3 us (12%)
  waiting for transfers between devices  7.29 us (8%)
    all_to_all x3, blocking collectives, peaks_of(): lax.all_to_all(peak.reshape(count, 1, 128), axis, 0, 0, tiled=True)  51.4 us
    all_to_all x1, blocking collectives, contract(): rows = lax.all_to_all(rows, 'draw', 0, 0, tiled=True)  7.95 us
    all_to_all x1, waiting for transfers between devices, contract(): sums = lax.all_to_all(sums, 'draw', 0, 0, tiled=True)  7.28 us
    ppermute x4, starting transfers between devices, exchange(): lax.ppermute(array, 'draw', [(d, d ^ distance) for d in range(draw_count)])  7.23 us
    pallas_call x1, Pallas kernels, contract(): pl.pallas_call(start_kernel, out_shape=(shape(3, slots, 128), shape(draw_...  4.28 us
    all_to_all x1, starting transfers between devices, contract(): sums = lax.all_to_all(sums, 'draw', 0, 0, tiled=True)  4.12 us
    pallas_call x1, Pallas kernels, contract(): pl.pallas_call(final_kernel, out_shape=(shape(own, slots, slots), shape(m...  3.9 us
    pallas_call x1, Pallas kernels, contract(): pl.pallas_call(second_kernel, out_shape=(shape(own, slots, draws), state_...  1.89 us
  transfers between devices with their start and end apart: 5, of which 1 were waited for; matrix products, arithmetic and copies ran while one was open for 0% of the time, Pallas kernels for 5%

profile of v4, /device:TPU:1, one launch (start us, length us, event | category | flops | bytes accessed | tf_op | source)
XLA Modules:
  0.0 90.4 jit_solution(6652695318748073017)
XLA Ops:
  0.6 3.3 %collective-permute-start = (f32[48,8,512]{2,1,0:T(8,128)}, f32[48,8,512]{2,1,0:T(8,128)S(1)}, u32[]{:S(2)}, u32[]{:S(2)}) collective-permute-start(f32[48,8,512]{2,1,0:T(8,128)} %nu_hbm.1), channel_id=1, source_target_pairs={{0,1},{1,0},{2,3},{3,2},{4,5},{5,4},{6,7},{7,6},{8,9},{9,8},{10,11... | collective-permute-start | bytes 2359304 | tf_op jit(solution)/shard_map/ppermute | solution.py:349
  3.9 4.3 %start.1 = (f32[3,56,128]{2,1,0:T(8,128)S(1)}, f32[8,32,128]{2,1,0:T(8,128)}, f32[48,8,512]{2,1,0:T(8,128)S(1)}, bf16[6,56,48]{2,1,0:T(8,128)(2,1)S(1)}) custom-call(s32[48]{0:T(128)} %counts_hbm.1, f32[8]{0:T(128)} %sigma_hbm.1, f32[48,56]{1,0:T(8,128)} %log_share_hbm.1, f32[48,8,56]{2,1,0:T(8,128)} %bitcast.19, f32[48,8,512]{2,1,0:T(8,128)} %nu_hbm.1), custom_call_target="tpu_custom_call" | custom-call | tf_op jit(solution)/shard_map/start/pallas_call | solution.py:357
  8.2 0.0 collective-permute-done.partner_ref
  8.3 0.1 collective-permute-start.1
  8.4 1.9 %collective-permute-start.2 = (f32[2,6,8,512]{3,2,1,0:T(8,128)S(1)}, f32[2,6,8,512]{3,2,1,0:T(8,128)S(1)}, u32[]{:S(2)}, u32[]{:S(2)}) collective-permute-start(f32[2,6,8,512]{3,2,1,0:T(8,128)S(1)} %get-tuple-element.27), channel_id=1, source_target_pairs={{0,4},{1,5},{2,6},{3,7},{4,0},{5,1},{6,2},{7,3},{8,12},{9,13},{10,... | collective-permute-start | bytes 589832 | tf_op jit(solution)/shard_map/ppermute | solution.py:349
  10.3 1.9 %collective-permute-start.3 = (f32[2,6,8,512]{3,2,1,0:T(8,128)S(1)}, f32[2,6,8,512]{3,2,1,0:T(8,128)S(1)}, u32[]{:S(2)}, u32[]{:S(2)}) collective-permute-start(f32[2,6,8,512]{3,2,1,0:T(8,128)S(1)} %get-tuple-element.28), channel_id=1, source_target_pairs={{0,6},{1,7},{2,4},{3,5},{4,2},{5,3},{6,0},{7,1},{8,14},{9,15},{10,... | collective-permute-start | bytes 589832 | tf_op jit(solution)/shard_map/ppermute | solution.py:349
  12.2 4.1 %all-to-all-start = ((f32[8,32,128]{2,1,0:T(8,128)}), f32[8,32,128]{2,1,0:T(8,128)S(1)}, u32[]{:S(2)}, u32[]{:S(2)}) async-start(f32[8,32,128]{2,1,0:T(8,128)} %get-tuple-element.20), calls=%async_computation | async-start | bytes 262144 | tf_op jit(solution)/shard_map/all_to_all | solution.py:389
  16.3 0.1 keep.1.refs_2_
  16.4 7.3 %all-to-all-done.refs_0_ = f32[8,32,128]{2,1,0:T(8,128)S(1)} async-done(((f32[8,32,128]{2,1,0:T(8,128)}), f32[8,32,128]{2,1,0:T(8,128)S(1)}, u32[]{:S(2)}, u32[]{:S(2)}) %all-to-all-start) | async-done | bytes 131104 | tf_op jit(solution)/shard_map/all_to_all | solution.py:389
  23.7 0.2 change.1
  23.9 19.6 %all_to_all.25 = f32[32,1,128]{2,1,0:T(1,128)S(1)} all-to-all(f32[32,1,128]{2,1,0:T(1,128)S(1)} %bitcast.18), channel_id=1, replica_groups=mesh['mkt'=32,'draw'=8] {'mkt'}, dimensions={0} | all-to-all | bytes 32768 | tf_op jit(solution)/shard_map/all_to_all | solution.py:353
  43.5 0.0 collective-permute-done.1.refs_0_
  43.5 0.0 collective-permute-done.2.refs_1_
  43.5 0.0 collective-permute-done.3.refs_2_
  43.5 1.9 %second.1 = (f32[6,56,4096]{2,1,0:T(8,128)S(1)}, f32[5,56,8]{2,1,0:T(8,128)S(1)}, f32[256,128]{1,0:T(8,128)S(1)}) custom-call(f32[32,128]{1,0:T(8,128)S(1)} %bitcast.15, f32[5,56,8]{2,1,0:T(8,128)S(1)} %get-tuple-element.23.state_ref, bf16[6,56,48]{2,1,0:T(8,128)(2,1)S(1)} %get-tuple-element.24.left_ref, f32[48,8,512]{2,1,0:T(8,128)S(1)} %get-tuple-element.25.nu_ref, ...), custom_call_target="tpu_custom_call" | custom-call | tf_op jit(solution)/shard_map/second/pallas_call | solution.py:407
  45.4 20.0 %all_to_all.26 = f32[256,1,128]{2,1,0:T(1,128)S(1)} all-to-all(f32[256,1,128]{2,1,0:T(1,128)S(1)} %bitcast.14), channel_id=1, replica_groups=mesh['mkt'=32,'draw'=8] {'mkt','draw'}, dimensions={0} | all-to-all | bytes 262144 | tf_op jit(solution)/shard_map/all_to_all | solution.py:353
  65.4 1.3 %third.1 = (f32[5,56,8]{2,1,0:T(8,128)S(1)}, f32[8,16,128]{2,1,0:T(8,128)S(1)}) custom-call(f32[256,128]{1,0:T(8,128)S(1)} %bitcast.13, f32[5,56,8]{2,1,0:T(8,128)S(1)} %get-tuple-element.30.state_ref, f32[6,56,4096]{2,1,0:T(8,128)S(1)} %get-tuple-element.31.raised_ref), custom_call_target="tpu_custom_call" | custom-call | tf_op jit(solution)/shard_map/third/pallas_call | solution.py:416
  66.8 7.9 %all_to_all.27.rows_ref = f32[8,16,128]{2,1,0:T(8,128)S(1)} all-to-all(f32[8,16,128]{2,1,0:T(8,128)S(1)} %get-tuple-element.32), channel_id=1, replica_groups=mesh['mkt'=32,'draw'=8] {'draw'}, dimensions={0} | all-to-all | bytes 131072 | tf_op jit(solution)/shard_map/all_to_all | solution.py:425
  74.7 0.1 join.1
  74.8 11.7 %all_to_all.28 = f32[32,1,128]{2,1,0:T(1,128)S(1)} all-to-all(f32[32,1,128]{2,1,0:T(1,128)S(1)} %bitcast.17), channel_id=1, replica_groups=mesh['mkt'=32,'draw'=8] {'mkt'}, dimensions={0} | all-to-all | bytes 32768 | tf_op jit(solution)/shard_map/all_to_all | solution.py:353
  86.5 3.9 %final.1 = (f32[6,56,56]{2,1,0:T(8,128)}, f32[48,56]{1,0:T(8,128)}, f32[3]{0:T(128)}) custom-call(f32[32,128]{1,0:T(8,128)S(1)} %bitcast.16, f32[5,56,8]{2,1,0:T(8,128)S(1)} %get-tuple-element.33.state_ref, f32[8,16,128]{2,1,0:T(8,128)S(1)} %all_to_all.27.rows_ref, f32[6,56,4096]{2,1,0:T(8,128)S(1)} %get-tuple-element.31.raised_ref), custom_call_target="tpu_custom_call" | custom-call | tf_op jit(solution)/shard_map/final/pallas_call | solution.py:434
  (1 shorter events, 0.0 us)
Async XLA Ops:
  0.6 7.6 %collective-permute-start = (f32[48,8,512]{2,1,0:T(8,128)}, f32[48,8,512]{2,1,0:T(8,128)S(1)}, u32[]{:S(2)}, u32[]{:S(2)}) collective-permute-start(f32[48,8,512]{2,1,0:T(8,128)} %nu_hbm.1), channel_id=1, source_target_pairs={{0,1},{1,0},{2,3},{3,2},{4,5},{5,4},{6,7},{7,6},{8,9},{9,8},{10,11... | collective-permute-start | bytes 2359304 | tf_op jit(solution)/shard_map/ppermute | solution.py:349
  8.3 35.2 %collective-permute-start.1 = (f32[2,6,8,512]{3,2,1,0:T(8,128)S(1)}, f32[2,6,8,512]{3,2,1,0:T(8,128)S(1)}, u32[]{:S(2)}, u32[]{:S(2)}) collective-permute-start(f32[2,6,8,512]{3,2,1,0:T(8,128)S(1)} %get-tuple-element.26), channel_id=1, source_target_pairs={{0,2},{1,3},{2,0},{3,1},{4,6},{5,7},{6,4},{7,5},{8,10},{9,11},{10,... | collective-permute-start | bytes 589832 | tf_op jit(solution)/shard_map/ppermute | solution.py:349
  8.4 35.1 %collective-permute-start.2 = (f32[2,6,8,512]{3,2,1,0:T(8,128)S(1)}, f32[2,6,8,512]{3,2,1,0:T(8,128)S(1)}, u32[]{:S(2)}, u32[]{:S(2)}) collective-permute-start(f32[2,6,8,512]{3,2,1,0:T(8,128)S(1)} %get-tuple-element.27), channel_id=1, source_target_pairs={{0,4},{1,5},{2,6},{3,7},{4,0},{5,1},{6,2},{7,3},{8,12},{9,13},{10,... | collective-permute-start | bytes 589832 | tf_op jit(solution)/shard_map/ppermute | solution.py:349
  10.3 33.2 %collective-permute-start.3 = (f32[2,6,8,512]{3,2,1,0:T(8,128)S(1)}, f32[2,6,8,512]{3,2,1,0:T(8,128)S(1)}, u32[]{:S(2)}, u32[]{:S(2)}) collective-permute-start(f32[2,6,8,512]{3,2,1,0:T(8,128)S(1)} %get-tuple-element.28), channel_id=1, source_target_pairs={{0,6},{1,7},{2,4},{3,5},{4,2},{5,3},{6,0},{7,1},{8,14},{9,15},{10,... | collective-permute-start | bytes 589832 | tf_op jit(solution)/shard_map/ppermute | solution.py:349
  12.2 11.5 %all-to-all-start = ((f32[8,32,128]{2,1,0:T(8,128)}), f32[8,32,128]{2,1,0:T(8,128)S(1)}, u32[]{:S(2)}, u32[]{:S(2)}) async-start(f32[8,32,128]{2,1,0:T(8,128)} %get-tuple-element.20), calls=%async_computation | async-start | bytes 262144 | tf_op jit(solution)/shard_map/all_to_all | solution.py:389
